TPU v7x, 256 devices: a whole 4x4x8 slice. The times are simulated.
256 devices in a mesh: rep: 32 (over z_hi, y, x), dom: 8 (over z_lo, core).
Axes of the slice: x: 4, y: 4, z: 8 (z_hi: 2, z_lo: 4; z = z_hi * 4 + z_lo), core: 2. Of those that a mesh axis runs over, the one named last changes fastest.
Arguments:
- protein_pos: float32 [3, 524288], P(None, ('rep', 'dom')), parts along dimension 1, may hold values from -4 to 4, as said below
- protein_vel: float32 [3, 524288], P(None, ('rep', 'dom')), parts along dimension 1, may hold values from -3 to 3
- inv_mass: float32 [524288], P(('rep', 'dom')), parts along dimension 0, may hold values from 0.0625 to 1
- bond_atoms: int32 [2, 327680], P(None, ('rep', 'dom')), parts along dimension 1, may hold values from 0 to 2047, as said below
- left_atoms: int32 [98304], P(('rep', 'dom')), parts along dimension 0, may hold values from 0 to 2047, as said below
- right_atoms: int32 [98304], P(('rep', 'dom')), parts along dimension 0, may hold values from 0 to 2047, as said below
- water_pos: float32 [9, 262144], P(None, ('rep', 'dom')), parts along dimension 1, may hold values from -3.2 to 3.2, as said below
- water_vel: float32 [9, 262144], P(None, ('rep', 'dom')), parts along dimension 1, may hold values from -3 to 3
Outputs:
- protein_velocity: float32 [3, 524288], P(None, ('rep', 'dom')), parts along dimension 1
- water_velocity: float32 [9, 262144], P(None, ('rep', 'dom')), parts along dimension 1
There are 32 independent parts, one for each index of `rep`. A program takes and returns all parts, laid end to end along the dimension named above; each array names one. Nothing has to cross between parts.
Inputs may be any that keep to these rules, and one draw needn't show every extreme that they name: `bond_atoms`: indices within the domain's block of 2048 atoms; each column joins two different atoms; together with the cross bonds the bonds form a forest. `left_atoms`: distinct indices within the domain's block, none of them in right_atoms. `right_atoms`: distinct indices within the domain's block. `protein_pos`: every bond and every cross bond joins atoms 0.1 to 0.15 apart. `water_pos`: each column holds one rigid water: oxygen, then two hydrogens, 0.09572 from the oxygen and 0.15139 from each other.
All inputs are finite; a program needn't handle non-finite values.
Results may differ from a plain program's by a relative error of at most 0.0003.
Values sent between devices are 32-bit elements; how exact they have to be, the bound alone decides.
A program may use at most 64 MiB of HBM per device.

v0:
```python
import math

import jax
import jax.numpy as jnp
from jax import lax
from jax.sharding import PartitionSpec as P

ORDER = 4
ITER = 2


time_step = 0.002
mass_oxygen = 15.9994
mass_hydrogen = 1.008
oxygen_hydrogen = 0.09572
hydrogen_pair = 0.15139
total_mass = mass_oxygen + 2.0 * mass_hydrogen
half_pair = 0.5 * hydrogen_pair
water_height = math.sqrt(oxygen_hydrogen * oxygen_hydrogen - half_pair * half_pair)
oxygen_reach = 2.0 * mass_hydrogen * water_height / total_mass
hydrogen_reach = water_height - oxygen_reach


def shifted(value, axis, steps):
    count = lax.axis_size(axis)
    pairs = [(source, (source + steps) % count) for source in range(count)]
    return lax.ppermute(value, axis, pairs)


def cross_product(left, right):
    return jnp.stack(
        [
            left[1] * right[2] - left[2] * right[1],
            left[2] * right[0] - left[0] * right[2],
            left[0] * right[1] - left[1] * right[0],
        ]
    )


def inner(left, right):
    return jnp.sum(left * right, axis=0)


def settle(before, after):
    old_oxygen, old_first, old_second = (before[0:3], before[3:6], before[6:9])
    new_oxygen, new_first, new_second = (after[0:3], after[3:6], after[6:9])
    center = (mass_oxygen * new_oxygen + mass_hydrogen * (new_first + new_second)) / total_mass
    old_b = old_first - old_oxygen
    old_c = old_second - old_oxygen
    rel_a = new_oxygen - center
    rel_b = new_first - center
    rel_c = new_second - center
    normal = cross_product(old_b, old_c)
    side = cross_product(rel_a, normal)
    upward = cross_product(normal, side)
    axis_z = normal / jnp.sqrt(inner(normal, normal))
    axis_x = side / jnp.sqrt(inner(side, side))
    axis_y = upward / jnp.sqrt(inner(upward, upward))
    oldb_x = inner(axis_x, old_b)
    oldb_y = inner(axis_y, old_b)
    oldc_x = inner(axis_x, old_c)
    oldc_y = inner(axis_y, old_c)
    newa_z = inner(axis_z, rel_a)
    newb_x = inner(axis_x, rel_b)
    newb_y = inner(axis_y, rel_b)
    newb_z = inner(axis_z, rel_b)
    newc_x = inner(axis_x, rel_c)
    newc_y = inner(axis_y, rel_c)
    newc_z = inner(axis_z, rel_c)
    sin_phi = newa_z / oxygen_reach
    cos_phi = jnp.sqrt(1.0 - sin_phi * sin_phi)
    sin_psi = (newb_z - newc_z) / (2.0 * half_pair * cos_phi)
    cos_psi = jnp.sqrt(1.0 - sin_psi * sin_psi)
    rest_ay = oxygen_reach * cos_phi
    rest_bx = -half_pair * cos_psi
    lowered = -hydrogen_reach * cos_phi
    tilted = half_pair * sin_psi * sin_phi
    rest_by = lowered - tilted
    rest_cy = lowered + tilted
    alpha = rest_bx * (oldb_x - oldc_x) + oldb_y * rest_by + oldc_y * rest_cy
    beta = rest_bx * (oldc_y - oldb_y) + oldb_x * rest_by + oldc_x * rest_cy
    gamma = oldb_x * newb_y - newb_x * oldb_y + oldc_x * newc_y - newc_x * oldc_y
    summed = alpha * alpha + beta * beta
    sin_theta = (alpha * gamma - beta * jnp.sqrt(summed - gamma * gamma)) / summed
    cos_theta = jnp.sqrt(1.0 - sin_theta * sin_theta)
    final_ax = -rest_ay * sin_theta
    final_ay = rest_ay * cos_theta
    final_bx = rest_bx * cos_theta - rest_by * sin_theta
    final_by = rest_bx * sin_theta + rest_by * cos_theta
    final_cx = -rest_bx * cos_theta - rest_cy * sin_theta
    final_cy = -rest_bx * sin_theta + rest_cy * cos_theta
    oxygen = center + axis_x * final_ax + axis_y * final_ay + axis_z * newa_z
    first = center + axis_x * final_bx + axis_y * final_by + axis_z * newb_z
    second = center + axis_x * final_cx + axis_y * final_cy + axis_z * newc_z
    return jnp.concatenate([oxygen, first, second], axis=0)


def solve_bonds(old_ext, moved_ext, mass_ext, first, second, count, atom_field):
    diff = old_ext[:, first] - old_ext[:, second]
    length = jnp.sqrt(inner(diff, diff))
    unit = diff / length
    scale = 1.0 / jnp.sqrt(mass_ext[first] + mass_ext[second])
    delta = jnp.zeros_like(moved_ext)
    rhs = scale * (inner(unit, moved_ext[:, first] - moved_ext[:, second]) - length)
    for round_index in range(ITER + 1):
        if round_index > 0:
            now = moved_ext + delta
            gap = now[:, first] - now[:, second]
            target = jnp.sqrt(2.0 * length * length - inner(gap, gap))
            rhs = scale * (length - target)
        total = rhs
        current = rhs
        for order_index in range(ORDER):
            field = atom_field(unit * (scale * current), True)
            current = current - scale * inner(unit, field[:, first] - field[:, second])
            total = total + current
        if round_index == ITER:
            return delta[:, :count] - atom_field(unit * (scale * total), False)
        delta = delta - atom_field(unit * (scale * total), True)


def on_device(
    protein_pos, protein_vel, inv_mass, bond_atoms, left_atoms, right_atoms, water_pos, water_vel
):
    count = protein_pos.shape[1]
    halo = left_atoms.shape[0]
    moved = protein_pos + time_step * protein_vel
    slots = jnp.arange(halo, dtype=jnp.int32)
    cap_data = jnp.concatenate(
        [protein_pos[:, left_atoms], moved[:, left_atoms], inv_mass[left_atoms][None]], axis=0
    )
    caps = shifted(cap_data, "dom", -1)
    old_ext = jnp.concatenate([protein_pos, caps[0:3]], axis=1)
    moved_ext = jnp.concatenate([moved, caps[3:6]], axis=1)
    mass_ext = jnp.concatenate([inv_mass, caps[6]])
    first = jnp.concatenate([bond_atoms[0], right_atoms])
    second = jnp.concatenate([bond_atoms[1], count + slots])

    def atom_field(weighted, edges):
        force = (
            jnp.zeros((3, count + halo), jnp.float32)
            .at[:, first]
            .add(weighted)
            .at[:, second]
            .add(-weighted)
        )
        returned = shifted(force[:, count:], "dom", 1)
        own_field = inv_mass * force[:, :count].at[:, left_atoms].add(returned)
        if edges:
            edge_field = shifted(own_field[:, left_atoms], "dom", -1)
            return jnp.concatenate([own_field, edge_field], axis=1)
        return own_field

    water_moved = water_pos + time_step * water_vel
    settled = settle(water_pos, water_moved)
    water_velocity = water_vel + (settled - water_moved) / time_step
    delta = solve_bonds(old_ext, moved_ext, mass_ext, first, second, count, atom_field)
    protein_velocity = protein_vel + delta / time_step
    return (protein_velocity, water_velocity)


def solution(mesh):
    in_specs = (
        P(None, ("rep", "dom")),
        P(None, ("rep", "dom")),
        P(("rep", "dom")),
        P(None, ("rep", "dom")),
        P(("rep", "dom")),
        P(("rep", "dom")),
        P(None, ("rep", "dom")),
        P(None, ("rep", "dom")),
    )
    out_specs = (P(None, ("rep", "dom")), P(None, ("rep", "dom")))
    return jax.shard_map(
        on_device, mesh=mesh, in_specs=in_specs, out_specs=out_specs, check_vma=False
    )
```

profile of v0, /device:TPU:1, one launch (start us, length us, event | category | flops | bytes accessed | tf_op | source)
XLA Modules:
  0.0 788.1 jit_solution(10719165229786931957)
XLA Ops:
  11.7 9.1 %gather_fusion.6 = f32[1664]{0:T(1024)S(1)} fusion(f32[2432]{0:T(1024)S(1)} %pad_maximum_fusion.18, s32[2048]{0:T(1024)S(1)} %pad_clamp_fusion), kind=kCustom, calls=%fused_computation.6 | custom fusion | bytes 19968 | tf_op jit(solution)/shard_map/gather | solution.py:102
  20.8 9.1 %gather_fusion.5 = f32[1664]{0:T(1024)S(1)} fusion(f32[2432]{0:T(1024)S(1)} %pad_maximum_fusion.18, s32[2048]{0:T(1024)S(1)} %pad_clamp_fusion.1), kind=kCustom, calls=%fused_computation.5 | custom fusion | bytes 19968 | tf_op jit(solution)/shard_map/gather | solution.py:102
  30.2 4.2 gather_fusion.4
  34.4 4.2 gather_fusion.3
  39.0 4.2 gather_fusion.8
  43.2 4.2 gather_fusion.7
  49.7 13.0 %scatter_custom_fusion = f32[3,2432]{0,1:T(8,128)S(1)} fusion(s32[1664]{0:T(1024)S(1)} %get-tuple-element.68, f32[]{:T(128)} %constant.17.clone.1, f32[1664]{0:T(1024)S(1)} %get-tuple-element.49, f32[1664,3]{1,0:T(8,128)S(1)} %get-tuple-element.53, f32[1664]{0:T(1024)S(1)} %sqrt.199), kind=kCustom, calls=%fused_computation.185 | custom fusion | flops 14976 | bytes 897540 | tf_op jit(solution)/shard_map/scatter-add | solution.py:143
  62.6 13.3 %scatter_custom_fusion.1 = f32[3,2432]{0,1:T(8,128)S(1)} fusion(f32[3,2432]{0,1:T(8,128)S(1)} %scatter_custom_fusion, s32[1664]{0:T(1024)S(1)} %get-tuple-element.69, f32[1664]{0:T(1024)S(1)} %get-tuple-element.49, f32[1664,3]{1,0:T(8,128)S(1)} %get-tuple-element.53, f32[1664]{0:T(1024)S(1)} %sqrt.199), kind=kCustom, calls=%fused_computation.125 | custom fusion | flops 19968 | bytes 897536 | tf_op jit(solution)/shard_map/scatter-add | solution.py:145
  85.2 6.0 collective-permute-start.2
  95.7 4.2 gather_fusion.10
  101.6 13.0 %scatter_custom_fusion.3 = f32[3,2432]{0,1:T(8,128)S(1)} fusion(s32[1664]{0:T(1024)S(1)} %get-tuple-element.68, f32[]{:T(128)} %constant.17.clone.1, f32[1664]{0:T(1024)S(1)} %fusion.163, f32[1664,3]{1,0:T(8,128)S(1)} %get-tuple-element.53, f32[1664]{0:T(1024)S(1)} %sqrt.199), kind=kCustom, calls=%fused_computation.182 | custom fusion | flops 14976 | bytes 897540 | tf_op jit(solution)/shard_map/scatter-add | solution.py:143
  114.6 13.3 %scatter_custom_fusion.4 = f32[3,2432]{0,1:T(8,128)S(1)} fusion(f32[3,2432]{0,1:T(8,128)S(1)} %scatter_custom_fusion.3, s32[1664]{0:T(1024)S(1)} %get-tuple-element.69, f32[1664]{0:T(1024)S(1)} %fusion.163, f32[1664,3]{1,0:T(8,128)S(1)} %get-tuple-element.53, f32[1664]{0:T(1024)S(1)} %sqrt.199), kind=kCustom, calls=%fused_computation.123 | custom fusion | flops 19968 | bytes 897536 | tf_op jit(solution)/shard_map/scatter-add | solution.py:145
  136.4 5.0 collective-permute-start.4
  145.8 4.2 gather_fusion.13
  151.8 13.0 %scatter_custom_fusion.6 = f32[3,2432]{0,1:T(8,128)S(1)} fusion(s32[1664]{0:T(1024)S(1)} %get-tuple-element.68, f32[]{:T(128)} %constant.17.clone.1, f32[1664]{0:T(1024)S(1)} %fusion.167, f32[1664,3]{1,0:T(8,128)S(1)} %get-tuple-element.53, f32[1664]{0:T(1024)S(1)} %sqrt.199), kind=kCustom, calls=%fused_computation.179 | custom fusion | flops 14976 | bytes 897540 | tf_op jit(solution)/shard_map/scatter-add | solution.py:143
  164.7 13.3 %scatter_custom_fusion.7 = f32[3,2432]{0,1:T(8,128)S(1)} fusion(f32[3,2432]{0,1:T(8,128)S(1)} %scatter_custom_fusion.6, s32[1664]{0:T(1024)S(1)} %get-tuple-element.69, f32[1664]{0:T(1024)S(1)} %fusion.167, f32[1664,3]{1,0:T(8,128)S(1)} %get-tuple-element.53, f32[1664]{0:T(1024)S(1)} %sqrt.199), kind=kCustom, calls=%fused_computation.121 | custom fusion | flops 19968 | bytes 897536 | tf_op jit(solution)/shard_map/scatter-add | solution.py:145
  186.2 5.0 collective-permute-start.6
  195.7 4.2 gather_fusion.16
  201.6 13.0 %scatter_custom_fusion.9 = f32[3,2432]{0,1:T(8,128)S(1)} fusion(s32[1664]{0:T(1024)S(1)} %get-tuple-element.68, f32[]{:T(128)} %constant.17.clone.1, f32[1664]{0:T(1024)S(1)} %fusion.158, f32[1664,3]{1,0:T(8,128)S(1)} %get-tuple-element.53, f32[1664]{0:T(1024)S(1)} %sqrt.199), kind=kCustom, calls=%fused_computation.176 | custom fusion | flops 14976 | bytes 897540 | tf_op jit(solution)/shard_map/scatter-add | solution.py:143
  214.6 13.3 %scatter_custom_fusion.10 = f32[3,2432]{0,1:T(8,128)S(1)} fusion(f32[3,2432]{0,1:T(8,128)S(1)} %scatter_custom_fusion.9, s32[1664]{0:T(1024)S(1)} %get-tuple-element.69, f32[1664]{0:T(1024)S(1)} %fusion.158, f32[1664,3]{1,0:T(8,128)S(1)} %get-tuple-element.53, f32[1664]{0:T(1024)S(1)} %sqrt.199), kind=kCustom, calls=%fused_computation.119 | custom fusion | flops 19968 | bytes 897536 | tf_op jit(solution)/shard_map/scatter-add | solution.py:145
  236.2 5.0 collective-permute-start.8
  245.7 4.2 gather_fusion.19
  251.6 13.0 %scatter_custom_fusion.12 = f32[3,2432]{0,1:T(8,128)S(1)} fusion(s32[1664]{0:T(1024)S(1)} %get-tuple-element.68, f32[]{:T(128)} %constant.17.clone.1, f32[1664]{0:T(1024)S(1)} %add_multiply_fusion.3, f32[1664,3]{1,0:T(8,128)S(1)} %get-tuple-element.53, f32[1664]{0:T(1024)S(1)} %sqrt.199), kind=kCustom, calls=%fused_computation.173 | custom fusion | flops 14976 | bytes 897540 | tf_op jit(solution)/shard_map/scatter-add | solution.py:143
  264.6 13.3 %scatter_custom_fusion.13 = f32[3,2432]{0,1:T(8,128)S(1)} fusion(f32[3,2432]{0,1:T(8,128)S(1)} %scatter_custom_fusion.12, s32[1664]{0:T(1024)S(1)} %get-tuple-element.69, f32[1664]{0:T(1024)S(1)} %add_multiply_fusion.3, f32[1664,3]{1,0:T(8,128)S(1)} %get-tuple-element.53, f32[1664]{0:T(1024)S(1)} %sqrt.199), kind=kCustom, calls=%fused_computation.117 | custom fusion | flops 19968 | bytes 897536 | tf_op jit(solution)/shard_map/scatter-add | solution.py:145
  286.2 5.0 collective-permute-start.10
  296.1 4.2 gather_fusion.22
  301.8 13.0 %scatter_custom_fusion.15 = f32[3,2432]{0,1:T(8,128)S(1)} fusion(s32[1664]{0:T(1024)S(1)} %get-tuple-element.68, f32[]{:T(128)} %constant.17.clone.1, f32[1664]{0:T(1024)S(1)} %get-tuple-element.47, f32[1664,3]{1,0:T(8,128)S(1)} %get-tuple-element.53, f32[1664]{0:T(1024)S(1)} %sqrt.199), kind=kCustom, calls=%fused_computation.170 | custom fusion | flops 14976 | bytes 897540 | tf_op jit(solution)/shard_map/scatter-add | solution.py:143
  314.8 13.3 %scatter_custom_fusion.16 = f32[3,2432]{0,1:T(8,128)S(1)} fusion(f32[3,2432]{0,1:T(8,128)S(1)} %scatter_custom_fusion.15, s32[1664]{0:T(1024)S(1)} %get-tuple-element.69, f32[1664]{0:T(1024)S(1)} %get-tuple-element.47, f32[1664,3]{1,0:T(8,128)S(1)} %get-tuple-element.53, f32[1664]{0:T(1024)S(1)} %sqrt.199), kind=kCustom, calls=%fused_computation.115 | custom fusion | flops 19968 | bytes 897536 | tf_op jit(solution)/shard_map/scatter-add | solution.py:145
  336.8 6.2 collective-permute-start.12
  347.5 4.2 gather_fusion.25
  353.4 13.0 %scatter_custom_fusion.18 = f32[3,2432]{0,1:T(8,128)S(1)} fusion(s32[1664]{0:T(1024)S(1)} %get-tuple-element.68, f32[]{:T(128)} %constant.17.clone.1, f32[1664]{0:T(1024)S(1)} %fusion.164, f32[1664,3]{1,0:T(8,128)S(1)} %get-tuple-element.53, f32[1664]{0:T(1024)S(1)} %sqrt.199), kind=kCustom, calls=%fused_computation.167 | custom fusion | flops 14976 | bytes 897540 | tf_op jit(solution)/shard_map/scatter-add | solution.py:143
  366.4 13.3 %scatter_custom_fusion.19 = f32[3,2432]{0,1:T(8,128)S(1)} fusion(f32[3,2432]{0,1:T(8,128)S(1)} %scatter_custom_fusion.18, s32[1664]{0:T(1024)S(1)} %get-tuple-element.69, f32[1664]{0:T(1024)S(1)} %fusion.164, f32[1664,3]{1,0:T(8,128)S(1)} %get-tuple-element.53, f32[1664]{0:T(1024)S(1)} %sqrt.199), kind=kCustom, calls=%fused_computation.113 | custom fusion | flops 19968 | bytes 897536 | tf_op jit(solution)/shard_map/scatter-add | solution.py:145
  388.0 5.0 collective-permute-start.14
  397.4 4.2 gather_fusion.28
  403.4 13.0 %scatter_custom_fusion.21 = f32[3,2432]{0,1:T(8,128)S(1)} fusion(s32[1664]{0:T(1024)S(1)} %get-tuple-element.68, f32[]{:T(128)} %constant.17.clone.1, f32[1664]{0:T(1024)S(1)} %fusion.168, f32[1664,3]{1,0:T(8,128)S(1)} %get-tuple-element.53, f32[1664]{0:T(1024)S(1)} %sqrt.199), kind=kCustom, calls=%fused_computation.164 | custom fusion | flops 14976 | bytes 897540 | tf_op jit(solution)/shard_map/scatter-add | solution.py:143
  416.3 13.3 %scatter_custom_fusion.22 = f32[3,2432]{0,1:T(8,128)S(1)} fusion(f32[3,2432]{0,1:T(8,128)S(1)} %scatter_custom_fusion.21, s32[1664]{0:T(1024)S(1)} %get-tuple-element.69, f32[1664]{0:T(1024)S(1)} %fusion.168, f32[1664,3]{1,0:T(8,128)S(1)} %get-tuple-element.53, f32[1664]{0:T(1024)S(1)} %sqrt.199), kind=kCustom, calls=%fused_computation.111 | custom fusion | flops 19968 | bytes 897536 | tf_op jit(solution)/shard_map/scatter-add | solution.py:145
  438.1 5.0 collective-permute-start.16
  447.6 4.2 gather_fusion.31
  453.5 13.0 %scatter_custom_fusion.24 = f32[3,2432]{0,1:T(8,128)S(1)} fusion(s32[1664]{0:T(1024)S(1)} %get-tuple-element.68, f32[]{:T(128)} %constant.17.clone.1, f32[1664]{0:T(1024)S(1)} %fusion.159, f32[1664,3]{1,0:T(8,128)S(1)} %get-tuple-element.53, f32[1664]{0:T(1024)S(1)} %sqrt.199), kind=kCustom, calls=%fused_computation.161 | custom fusion | flops 14976 | bytes 897540 | tf_op jit(solution)/shard_map/scatter-add | solution.py:143
  466.5 13.3 %scatter_custom_fusion.25 = f32[3,2432]{0,1:T(8,128)S(1)} fusion(f32[3,2432]{0,1:T(8,128)S(1)} %scatter_custom_fusion.24, s32[1664]{0:T(1024)S(1)} %get-tuple-element.69, f32[1664]{0:T(1024)S(1)} %fusion.159, f32[1664,3]{1,0:T(8,128)S(1)} %get-tuple-element.53, f32[1664]{0:T(1024)S(1)} %sqrt.199), kind=kCustom, calls=%fused_computation.109 | custom fusion | flops 19968 | bytes 897536 | tf_op jit(solution)/shard_map/scatter-add | solution.py:145
  488.0 5.0 collective-permute-start.18
  497.5 4.2 gather_fusion.34
  503.4 13.0 %scatter_custom_fusion.27 = f32[3,2432]{0,1:T(8,128)S(1)} fusion(s32[1664]{0:T(1024)S(1)} %get-tuple-element.68, f32[]{:T(128)} %constant.17.clone.1, f32[1664]{0:T(1024)S(1)} %add_multiply_fusion.2, f32[1664,3]{1,0:T(8,128)S(1)} %get-tuple-element.53, f32[1664]{0:T(1024)S(1)} %sqrt.199), kind=kCustom, calls=%fused_computation.158 | custom fusion | flops 14976 | bytes 897540 | tf_op jit(solution)/shard_map/scatter-add | solution.py:143
  516.4 13.3 %scatter_custom_fusion.28 = f32[3,2432]{0,1:T(8,128)S(1)} fusion(f32[3,2432]{0,1:T(8,128)S(1)} %scatter_custom_fusion.27, s32[1664]{0:T(1024)S(1)} %get-tuple-element.69, f32[1664]{0:T(1024)S(1)} %add_multiply_fusion.2, f32[1664,3]{1,0:T(8,128)S(1)} %get-tuple-element.53, f32[1664]{0:T(1024)S(1)} %sqrt.199), kind=kCustom, calls=%fused_computation.107 | custom fusion | flops 19968 | bytes 897536 | tf_op jit(solution)/shard_map/scatter-add | solution.py:145
  538.0 5.0 collective-permute-start.20
  547.5 4.2 gather_fusion.37
  553.1 13.1 %scatter_custom_fusion.30 = f32[3,2432]{0,1:T(8,128)S(1)} fusion(s32[1664]{0:T(1024)} %copy-done.31, f32[]{:T(128)} %constant.17.clone.1, f32[1664]{0:T(1024)S(1)} %get-tuple-element.43, f32[1664,3]{1,0:T(8,128)S(1)} %get-tuple-element.53, f32[1664]{0:T(1024)S(1)} %sqrt.199), kind=kCustom, calls=%fused_computation.155 | custom fusion | flops 14976 | bytes 62976 | tf_op jit(solution)/shard_map/scatter-add | solution.py:143
  566.3 13.4 %scatter_custom_fusion.31 = f32[3,2432]{0,1:T(8,128)S(1)} fusion(f32[3,2432]{0,1:T(8,128)S(1)} %scatter_custom_fusion.30, s32[1664]{0:T(1024)} %copy-done.30, f32[1664]{0:T(1024)S(1)} %get-tuple-element.43, f32[1664,3]{1,0:T(8,128)S(1)} %get-tuple-element.53, f32[1664]{0:T(1024)S(1)} %sqrt.199), kind=kCustom, calls=%fused_computation.105 | custom fusion | flops 19968 | bytes 897536 | tf_op jit(solution)/shard_map/scatter-add | solution.py:145
  588.1 5.0 collective-permute-start.22
  597.6 4.2 gather_fusion.40
  603.5 13.1 %scatter_custom_fusion.33 = f32[3,2432]{0,1:T(8,128)S(1)} fusion(s32[1664]{0:T(1024)} %copy-done.31, f32[]{:T(128)} %constant.17.clone.1, f32[1664]{0:T(1024)S(1)} %fusion.165, f32[1664,3]{1,0:T(8,128)S(1)} %get-tuple-element.53, f32[1664]{0:T(1024)S(1)} %sqrt.199), kind=kCustom, calls=%fused_computation.152 | custom fusion | flops 14976 | bytes 62976 | tf_op jit(solution)/shard_map/scatter-add | solution.py:143
  616.6 13.4 %scatter_custom_fusion.34 = f32[3,2432]{0,1:T(8,128)S(1)} fusion(f32[3,2432]{0,1:T(8,128)S(1)} %scatter_custom_fusion.33, s32[1664]{0:T(1024)} %copy-done.30, f32[1664]{0:T(1024)S(1)} %fusion.165, f32[1664,3]{1,0:T(8,128)S(1)} %get-tuple-element.53, f32[1664]{0:T(1024)S(1)} %sqrt.199), kind=kCustom, calls=%fused_computation.103 | custom fusion | flops 19968 | bytes 897536 | tf_op jit(solution)/shard_map/scatter-add | solution.py:145
  638.3 5.0 collective-permute-start.24
  647.8 4.2 gather_fusion.43
  653.7 13.1 %scatter_custom_fusion.36 = f32[3,2432]{0,1:T(8,128)S(1)} fusion(s32[1664]{0:T(1024)} %copy-done.31, f32[]{:T(128)} %constant.17.clone.1, f32[1664]{0:T(1024)S(1)} %fusion.169, f32[1664,3]{1,0:T(8,128)S(1)} %get-tuple-element.53, f32[1664]{0:T(1024)S(1)} %sqrt.199), kind=kCustom, calls=%fused_computation.149 | custom fusion | flops 14976 | bytes 62976 | tf_op jit(solution)/shard_map/scatter-add | solution.py:143
  666.8 13.4 %scatter_custom_fusion.37 = f32[3,2432]{0,1:T(8,128)S(1)} fusion(f32[3,2432]{0,1:T(8,128)S(1)} %scatter_custom_fusion.36, s32[1664]{0:T(1024)} %copy-done.30, f32[1664]{0:T(1024)S(1)} %fusion.169, f32[1664,3]{1,0:T(8,128)S(1)} %get-tuple-element.53, f32[1664]{0:T(1024)S(1)} %sqrt.199), kind=kCustom, calls=%fused_computation.101 | custom fusion | flops 19968 | bytes 897536 | tf_op jit(solution)/shard_map/scatter-add | solution.py:145
  688.6 5.0 collective-permute-start.26
  698.1 4.2 gather_fusion.46
  704.0 13.1 %scatter_custom_fusion.39 = f32[3,2432]{0,1:T(8,128)S(1)} fusion(s32[1664]{0:T(1024)} %copy-done.31, f32[]{:T(128)} %constant.17.clone.1, f32[1664]{0:T(1024)S(1)} %fusion.160, f32[1664,3]{1,0:T(8,128)S(1)} %get-tuple-element.53, f32[1664]{0:T(1024)S(1)} %sqrt.199), kind=kCustom, calls=%fused_computation.146 | custom fusion | flops 14976 | bytes 62976 | tf_op jit(solution)/shard_map/scatter-add | solution.py:143
  717.1 13.4 %scatter_custom_fusion.40 = f32[3,2432]{0,1:T(8,128)S(1)} fusion(f32[3,2432]{0,1:T(8,128)S(1)} %scatter_custom_fusion.39, s32[1664]{0:T(1024)} %copy-done.30, f32[1664]{0:T(1024)S(1)} %fusion.160, f32[1664,3]{1,0:T(8,128)S(1)} %get-tuple-element.53, f32[1664]{0:T(1024)S(1)} %sqrt.199), kind=kCustom, calls=%fused_computation.99 | custom fusion | flops 19968 | bytes 897536 | tf_op jit(solution)/shard_map/scatter-add | solution.py:145
  738.9 5.0 collective-permute-start.28
  748.3 4.2 gather_fusion.49
  754.3 13.1 %scatter_custom_fusion.42 = f32[3,2432]{0,1:T(8,128)S(1)} fusion(s32[1664]{0:T(1024)} %copy-done.31, f32[]{:T(128)} %constant.17.clone.1, f32[1664]{0:T(1024)S(1)} %add_multiply_fusion.1, f32[1664,3]{1,0:T(8,128)S(1)} %get-tuple-element.53, f32[1664]{0:T(1024)S(1)} %sqrt.199), kind=kCustom, calls=%fused_computation.143 | custom fusion | flops 14976 | bytes 62976 | tf_op jit(solution)/shard_map/scatter-add | solution.py:143
  767.4 13.4 %scatter_custom_fusion.43 = f32[3,2432]{0,1:T(8,128)S(1)} fusion(f32[3,2432]{0,1:T(8,128)S(1)} %scatter_custom_fusion.42, s32[1664]{0:T(1024)} %copy-done.30, f32[1664]{0:T(1024)S(1)} %add_multiply_fusion.1, f32[1664,3]{1,0:T(8,128)S(1)} %get-tuple-element.53, f32[1664]{0:T(1024)S(1)} %sqrt.199), kind=kCustom, calls=%fused_computation.97 | custom fusion | flops 19968 | bytes 897536 | tf_op jit(solution)/shard_map/scatter-add | solution.py:145
  (371 shorter events, 224.9 us)
Async XLA Ops:
  1.3 581.0 %copy-start.44 = (s32[384]{0:T(512)}, s32[384]{0:T(512)S(1)}, u32[]{:S(2)}) copy-start(s32[384]{0:T(512)S(1)} %compare_select_fusion.2) | copy-start | bytes 4612
  7.2 4.5 collective-permute-start
  10.6 492.8 %copy-start.31 = (s32[1664]{0:T(1024)}, s32[1664]{0:T(1024)S(1)}, u32[]{:S(2)}) copy-start(s32[1664]{0:T(1024)S(1)} %get-tuple-element.68) | copy-start | bytes 19972
  10.6 505.8 %copy-start.30 = (s32[1664]{0:T(1024)}, s32[1664]{0:T(1024)S(1)}, u32[]{:S(2)}) copy-start(s32[1664]{0:T(1024)S(1)} %get-tuple-element.69) | copy-start | bytes 19972
  38.5 8.8 %copy-start.1 = (f32[1664,3]{1,0:T(8,128)S(1)}, f32[1664,3]{1,0:T(8,128)}, u32[]{:S(2)}) copy-start(f32[1664,3]{1,0:T(8,128)} %gather_fusion.4) | copy-start | bytes 59908
  75.9 3.7 collective-permute-start.1
  85.2 6.8 collective-permute-start.2
  127.9 2.7 collective-permute-start.3
  136.4 5.8 collective-permute-start.4
  178.0 2.7 collective-permute-start.5
  186.2 5.8 collective-permute-start.6
  227.9 2.7 collective-permute-start.7
  236.2 5.8 collective-permute-start.8
  277.9 2.7 collective-permute-start.9
  286.2 6.1 collective-permute-start.10
  292.4 7.9 %copy-start.22 = (f32[3,384]{1,0:T(4,128)}, f32[3,384]{1,0:T(4,128)S(1)}, u32[]{:S(2)}) copy-start(f32[3,384]{1,0:T(4,128)S(1)} %copy.161) | copy-start | bytes 13828
  328.1 3.3 collective-permute-start.11
  336.8 7.0 collective-permute-start.12
  379.7 2.7 collective-permute-start.13
  388.0 5.8 collective-permute-start.14
  429.6 2.7 collective-permute-start.15
  438.1 5.8 collective-permute-start.16
  479.8 2.7 collective-permute-start.17
  488.0 5.8 collective-permute-start.18
  516.4 13.4 %copy-start.4 = (f32[9,1024]{1,0:T(8,128)S(1)}, f32[9,1024]{1,0:T(8,128)}, u32[]{:S(2)}) copy-start(f32[9,1024]{1,0:T(8,128)} %param.14) | copy-start | bytes 110596
  516.4 13.4 %copy-start.5 = (f32[9,1024]{1,0:T(8,128)S(1)}, f32[9,1024]{1,0:T(8,128)}, u32[]{:S(2)}) copy-start(f32[9,1024]{1,0:T(8,128)} %param.15) | copy-start | bytes 110596
  529.7 2.7 collective-permute-start.19
  536.3 7.4 copy-start.23
  538.0 5.8 collective-permute-start.20
  579.7 2.7 collective-permute-start.21
  588.1 5.8 collective-permute-start.22
  593.7 36.4 %copy-start.15 = (f32[1,1024]{1,0:T(1,128)}, f32[1,1024]{1,0:T(1,128)S(1)}, u32[]{:S(2)}) copy-start(f32[1,1024]{1,0:T(1,128)S(1)} %get-tuple-element.34) | copy-start | bytes 12292
  593.7 36.4 %copy-start.17 = (f32[1,1024]{1,0:T(1,128)}, f32[1,1024]{1,0:T(1,128)S(1)}, u32[]{:S(2)}) copy-start(f32[1,1024]{1,0:T(1,128)S(1)} %get-tuple-element.38) | copy-start | bytes 12292
  630.1 2.7 collective-permute-start.23
  630.8 12.5 %copy-start.12 = (f32[1,1024]{1,0:T(1,128)}, f32[1,1024]{1,0:T(1,128)S(1)}, u32[]{:S(2)}) copy-start(f32[1,1024]{1,0:T(1,128)S(1)} %get-tuple-element.40) | copy-start | bytes 12292
  636.7 6.6 copy-start.16
  636.7 6.7 copy-start.18
  636.7 6.7 copy-start.28
  636.7 6.7 copy-start.29
  638.3 5.8 collective-permute-start.24
  666.8 13.5 %copy-start.9 = (f32[3,1024]{1,0:T(4,128)S(1)}, f32[3,1024]{1,0:T(4,128)}, u32[]{:S(2)}) copy-start(f32[3,1024]{1,0:T(4,128)} %get-tuple-element.57) | copy-start | bytes 36868
  666.8 13.5 %copy-start.11 = (f32[3,1024]{1,0:T(4,128)S(1)}, f32[3,1024]{1,0:T(4,128)}, u32[]{:S(2)}) copy-start(f32[3,1024]{1,0:T(4,128)} %get-tuple-element.58) | copy-start | bytes 36868
  666.8 13.5 %copy-start.13 = (f32[1,1024]{1,0:T(1,128)S(1)}, f32[1,1024]{1,0:T(1,128)}, u32[]{:S(2)}) copy-start(f32[1,1024]{1,0:T(1,128)} %copy-done.12) | copy-start | bytes 12292
  680.3 2.7 collective-permute-start.25
  681.7 11.8 %copy-start.24 = (f32[1024]{0:T(1024)}, f32[1024]{0:T(1024)S(1)}, u32[]{:S(2)}) copy-start(f32[1024]{0:T(1024)S(1)} %get-tuple-element.12) | copy-start | bytes 12292
  681.7 11.8 %copy-start.26 = (f32[1024]{0:T(1024)}, f32[1024]{0:T(1024)S(1)}, u32[]{:S(2)}) copy-start(f32[1024]{0:T(1024)S(1)} %get-tuple-element.13) | copy-start | bytes 12292
  686.6 7.0 copy-start.32
  686.6 7.0 copy-start.33
  686.6 7.0 copy-start.34
  686.6 7.0 copy-start.35
  686.6 7.0 copy-start.36
  686.6 7.0 copy-start.37
  686.6 7.0 copy-start.38
  686.6 7.0 copy-start.39
  688.6 5.8 collective-permute-start.26
  730.5 2.7 collective-permute-start.27
  736.9 7.0 copy-start.19
  736.9 7.0 copy-start.20
  736.9 7.0 copy-start.21
  736.9 7.0 copy-start.25
  736.9 6.9 copy-start.27
  736.9 6.9 copy-start.40
  738.9 5.8 collective-permute-start.28
  780.8 2.7 collective-permute-start.29
  (12 other events, 56.5 us)
where the time goes:
time: 801 us; the launch traced here: 788 us
  other arithmetic  482 us (60%)
  local copies, waits for them, and re-layouts  179 us (22%)
  starting transfers between devices  76.3 us (10%)
  waiting for transfers between devices  47.4 us (6%)
    scatter-add x30, other arithmetic, atom_field(): force = jnp.zeros((3, count + halo), jnp.float32).at[:, first].add(weight...  395 us
    gather x24, local copies, waits for them, and re-layouts, solve_bonds(): current = current - scale * inner(unit, field[:, first] - field[:, second])  88.8 us
    ppermute x30, starting transfers between devices, shifted(): return lax.ppermute(value, axis, pairs)  76.3 us
    scatter-add x15, other arithmetic, atom_field(): own_field = inv_mass * force[:, :count].at[:, left_atoms].add(returned)  54.2 us
    ppermute x30, waiting for transfers between devices, shifted(): return lax.ppermute(value, axis, pairs)  47.4 us
    reduce_sum x19, other arithmetic, inner(): return jnp.sum(left * right, axis=0)  27.5 us
    gather x2, local copies, waits for them, and re-layouts, solve_bonds(): scale = 1.0 / jnp.sqrt(mass_ext[first] + mass_ext[second])  18.2 us
    gather x27, local copies, waits for them, and re-layouts, atom_field(): edge_field = shifted(own_field[:, left_atoms], 'dom', -1)  16.8 us
  transfers between devices with their start and end apart: 30, of which 30 were waited for; matrix products, arithmetic and copies ran while one was open for 1% of the time, Pallas kernels for 0%

commit v1 on v0

v1 whole, which is shorter than its diff:
```python
import math

import jax
import jax.numpy as jnp
from jax import lax
from jax.experimental import pallas as pl
from jax.experimental.pallas import tpu as pltpu
from jax.sharding import PartitionSpec as P

ORDER = 4
ITER = 2

time_step = 0.002
mass_oxygen = 15.9994
mass_hydrogen = 1.008
oxygen_hydrogen = 0.09572
hydrogen_pair = 0.15139
total_mass = mass_oxygen + 2.0 * mass_hydrogen
half_pair = 0.5 * hydrogen_pair
water_height = math.sqrt(oxygen_hydrogen * oxygen_hydrogen - half_pair * half_pair)
oxygen_reach = 2.0 * mass_hydrogen * water_height / total_mass
hydrogen_reach = water_height - oxygen_reach

E = 20
S = 6
DIFF, DVEL, SCALE, MASS, PIDX, CONT, CIDX = 0, 3 * E, 6 * E, 7 * E, 8 * E, 9 * E, 10 * E
SPOS = 11 * E
SVEL, SMASS, SIDX = SPOS + 3 * S, SPOS + 6 * S, SPOS + 7 * S
ROWS = 272
f32, i32 = jnp.float32, jnp.int32


def take(table, lanes):
    return jnp.take_along_axis(table, lanes, axis=1, mode="promise_in_bounds")


def cross3(a, b):
    return (
        a[1] * b[2] - a[2] * b[1],
        a[2] * b[0] - a[0] * b[2],
        a[0] * b[1] - a[1] * b[0],
    )


def dot3(a, b):
    return a[0] * b[0] + a[1] * b[1] + a[2] * b[2]


def settle(old, vel):
    old_b = [old[3 + k] - old[k] for k in range(3)]
    old_c = [old[6 + k] - old[k] for k in range(3)]
    new_a = [time_step * vel[k] for k in range(3)]
    new_b = [old_b[k] + time_step * vel[3 + k] for k in range(3)]
    new_c = [old_c[k] + time_step * vel[6 + k] for k in range(3)]
    center = [
        (mass_oxygen * new_a[k] + mass_hydrogen * (new_b[k] + new_c[k])) / total_mass
        for k in range(3)
    ]
    rel_a = [new_a[k] - center[k] for k in range(3)]
    rel_b = [new_b[k] - center[k] for k in range(3)]
    rel_c = [new_c[k] - center[k] for k in range(3)]
    normal = cross3(old_b, old_c)
    side = cross3(rel_a, normal)
    upward = cross3(normal, side)

    def norm(vec):
        size = jnp.sqrt(dot3(vec, vec))
        return [part / size for part in vec]

    axis_z, axis_x, axis_y = norm(normal), norm(side), norm(upward)
    oldb_x, oldb_y = dot3(axis_x, old_b), dot3(axis_y, old_b)
    oldc_x, oldc_y = dot3(axis_x, old_c), dot3(axis_y, old_c)
    newa_z = dot3(axis_z, rel_a)
    newb_x, newb_y, newb_z = dot3(axis_x, rel_b), dot3(axis_y, rel_b), dot3(axis_z, rel_b)
    newc_x, newc_y, newc_z = dot3(axis_x, rel_c), dot3(axis_y, rel_c), dot3(axis_z, rel_c)
    sin_phi = newa_z / oxygen_reach
    cos_phi = jnp.sqrt(1.0 - sin_phi * sin_phi)
    sin_psi = (newb_z - newc_z) / (2.0 * half_pair * cos_phi)
    cos_psi = jnp.sqrt(1.0 - sin_psi * sin_psi)
    rest_ay = oxygen_reach * cos_phi
    rest_bx = -half_pair * cos_psi
    lowered = -hydrogen_reach * cos_phi
    tilted = half_pair * sin_psi * sin_phi
    rest_by = lowered - tilted
    rest_cy = lowered + tilted
    alpha = rest_bx * (oldb_x - oldc_x) + oldb_y * rest_by + oldc_y * rest_cy
    beta = rest_bx * (oldc_y - oldb_y) + oldb_x * rest_by + oldc_x * rest_cy
    gamma = oldb_x * newb_y - newb_x * oldb_y + oldc_x * newc_y - newc_x * oldc_y
    summed = alpha * alpha + beta * beta
    sin_theta = (alpha * gamma - beta * jnp.sqrt(summed - gamma * gamma)) / summed
    cos_theta = jnp.sqrt(1.0 - sin_theta * sin_theta)
    final_ax = -rest_ay * sin_theta
    final_ay = rest_ay * cos_theta
    final_bx = rest_bx * cos_theta - rest_by * sin_theta
    final_by = rest_bx * sin_theta + rest_by * cos_theta
    final_cx = -rest_bx * cos_theta - rest_cy * sin_theta
    final_cy = -rest_bx * sin_theta + rest_cy * cos_theta
    out = []
    for rel, along_x, along_y, along_z in (
        (rel_a, final_ax, final_ay, newa_z),
        (rel_b, final_bx, final_by, newb_z),
        (rel_c, final_cx, final_cy, newc_z),
    ):
        for k in range(3):
            out.append(axis_x[k] * along_x + axis_y[k] * along_y + axis_z[k] * along_z - rel[k])
    return [vel[k] + out[k] / time_step for k in range(9)]


def sort4(x):
    lane = lax.broadcasted_iota(i32, (8, 128), 1)
    sub = lax.broadcasted_iota(i32, (8, 128), 0)
    within = (lane << 5) | (sub << 2)
    x = list(x)
    for k in range(1, 13):
        for j in range(k - 1, -1, -1):
            if j < 2:
                for a in range(4):
                    b = a | (1 << j)
                    if a == b:
                        continue
                    low, high = jnp.minimum(x[a], x[b]), jnp.maximum(x[a], x[b])
                    if k == 12:
                        x[a], x[b] = low, high
                    elif k < 2:
                        x[a], x[b] = (low, high) if not (a >> k) & 1 else (high, low)
                    else:
                        up = ((within >> k) & 1) == 0
                        x[a], x[b] = jnp.where(up, low, high), jnp.where(up, high, low)
                continue
            first = ((within >> j) & 1) == 0
            if k == 12:
                keep_low = first
            else:
                keep_low = ((within >> j) & 1) == ((within >> k) & 1)
            for a in range(4):
                if j < 5:
                    step = 1 << (j - 2)
                    if step == 4:
                        other = pltpu.roll(x[a], 4, 0)
                    else:
                        other = jnp.where(
                            first, pltpu.roll(x[a], 8 - step, 0), pltpu.roll(x[a], step, 0)
                        )
                else:
                    other = take(x[a], lane ^ (1 << (j - 5)))
                x[a] = jnp.where(keep_low, jnp.minimum(x[a], other), jnp.maximum(x[a], other))
    return x


def gather_rows(tables, count, rows, lanes):
    outs = []
    for row_at, lane_at in zip(rows, lanes):
        hits = [row_at == r for r in range(count)]
        got = []
        for table in tables:
            acc = jnp.zeros((8, 128), table(0).dtype)
            for r in range(count):
                acc = jnp.where(hits[r], take(table(r), lane_at), acc)
            got.append(acc)
        outs.append(got)
    return outs


def row_of(ref, *base):
    def read(r):
        return jnp.broadcast_to(ref[base + (pl.ds(r, 1),)] if base else ref[pl.ds(r, 1), :], (8, 128))

    return read


def prepare(
    pos, vel, mass, bonds, left, right, wpos, wvel, block, local, wout,
    table, ends, keys, atoms, before, slots, water,
):
    lane = lax.broadcasted_iota(i32, (8, 128), 1)
    sub = lax.broadcasted_iota(i32, (8, 128), 0)
    for r in range(16):
        at = pl.ds(128 * r, 128)
        for k in range(3):
            table[k, pl.ds(r, 1)] = pos[pl.ds(k, 1), at]
            table[3 + k, pl.ds(r, 1)] = vel[pl.ds(k, 1), at]
        table[6, pl.ds(r, 1)] = mass[pl.ds(r, 1), :]
    for half in range(2):
        ends[pl.ds(16 * half + 8, 8), :] = jnp.full((8, 128), 2048, i32)
        for r in range(10):
            ends[pl.ds(16 * half + r, 1), :] = bonds[pl.ds(half, 1), pl.ds(128 * r, 128)]
    slots[...] = jnp.zeros((8, 128), i32)
    for r in range(3):
        slots[pl.ds(r, 1), :] = right[pl.ds(r, 1), :]
        slots[pl.ds(3 + r, 1), :] = left[pl.ds(r, 1), :]

    start = []
    for q in range(4):
        at = sub + 8 * q
        start.append((ends[pl.ds(8 * q, 8), :] << 12) | (at << 7) | lane)
    done = sort4(start)
    for q in range(4):
        before[pl.ds(8 * q, 8), :] = done[q]
    rows, lanes = [], []
    for q in range(3):
        n = jnp.minimum(lane * E + sub + 8 * q, 4095)
        rows.append(((n & 3) << 3) | ((n >> 2) & 7))
        lanes.append(n >> 5)
    key = [g[0] for g in gather_rows([row_of(before)], 32, rows, lanes)]
    for q in range(3):
        keys[pl.ds(8 * q, 8), :] = key[q]
    atom = [k >> 12 for k in key]
    twin = [(k & 4095) ^ 2048 for k in key]
    other = [
        g[0]
        for g in gather_rows([row_of(ends)], 26, [t >> 7 for t in twin], [t & 127 for t in twin])
    ]

    slot_atom = slots[...]
    own_atom = [(sub + 8 * q) * 128 + lane for q in range(2)]
    queries = [(other[q] << 12) | twin[q] for q in range(3)]
    queries += [(a << 12) | 4095 for a in [slot_atom] + own_atom]
    leaders = jnp.broadcast_to(keys[pl.ds(0, 1), :], (8, 128))
    found_row, found_lane, found_key = [], [], []
    for query in queries:
        low = jnp.zeros((8, 128), i32)
        for bit in (64, 32, 16, 8, 4, 2, 1):
            low = jnp.where(take(leaders, low + bit) <= query, low + bit, low)
        count = jnp.full((8, 128), -1, i32)
        best = jnp.full((8, 128), -1, i32)
        for r in range(E):
            seen = take(jnp.broadcast_to(keys[pl.ds(r, 1), :], (8, 128)), low)
            less = seen <= query
            count = jnp.where(less, count + 1, count)
            best = jnp.where(less, seen, best)
        found_row.append(count)
        found_lane.append(low)
        found_key.append(best)
    places = [found_row[q] * 128 + found_lane[q] for q in range(6)]
    slot_place = jnp.where((found_key[3] >> 12) == slot_atom, places[3], -1)
    for q in range(2):
        place = jnp.where((found_key[4 + q] >> 12) == own_atom[q], places[4 + q], -1)
        local[pl.ds(8 * q, 8), :] = place.astype(f32)

    high = lax.broadcasted_iota(i32, (16, 128), 0)
    code = lax.broadcasted_iota(i32, (16, 128), 1) + 1
    low_of = lax.broadcasted_iota(i32, (128, 128), 0)
    which = jnp.zeros((32, 128), f32)
    for r in range(S):
        here = slots[pl.ds(r, 1), :]
        mine = jnp.broadcast_to(here >> 7, (16, 128)) == high
        left_side = jnp.concatenate(
            [jnp.where(mine, code, 0).astype(f32), jnp.where(mine, r + 1, 0).astype(f32)], axis=0
        )
        right_side = jnp.where(jnp.broadcast_to(here & 127, (128, 128)) == low_of, 1.0, 0.0)
        which = which + lax.dot_general(
            left_side.astype(jnp.bfloat16),
            right_side.astype(jnp.bfloat16),
            (((1,), (1,)), ((), ())),
            preferred_element_type=f32,
        )
    local[pl.ds(16, 16), :] = jnp.where(
        which[0:16] > 0.0, which[16:32] * 128.0 + which[0:16] - 129.0, -1.0
    )

    for q in range(3):
        atoms[pl.ds(8 * q, 8), :] = atom[q]
    before[pl.ds(0, 1), :] = pltpu.roll(atoms[pl.ds(E - 1, 1), :], 1, 1)
    before[pl.ds(1, E - 1), :] = atoms[pl.ds(0, E - 1), :]
    own_rows, own_lanes = [a >> 7 for a in atom], [a & 127 for a in atom]
    tables = [row_of(table, k) for k in range(7)] + [row_of(local.at[pl.ds(16, 16)])]
    own = gather_rows(tables, 16, own_rows, own_lanes)
    far = gather_rows(tables[:7], 16, [a >> 7 for a in other], [a & 127 for a in other])
    for q in range(3):
        size = min(8, E - 8 * q)

        def put(base, value):
            block[pl.ds(base + 8 * q, size), :] = value[0:size]

        for k in range(3):
            put(DIFF + E * k, own[q][k] - far[q][k])
            put(DVEL + E * k, own[q][3 + k] - far[q][3 + k])
        put(SCALE, 1.0 / jnp.sqrt(own[q][6] + far[q][6]))
        put(MASS, own[q][6])
        put(PIDX, places[q].astype(f32))
        same = before[pl.ds(8 * q, 8), :] == atom[q]
        if q == 0:
            same = same & ((lane > 0) | (sub > 0))
        put(CONT, jnp.where(same, 1.0, 0.0))
        put(CIDX, own[q][7])
    at_slots = gather_rows(tables[:7], 16, [slot_atom >> 7], [slot_atom & 127])[0]
    for k in range(7):
        block[pl.ds(SPOS + S * k, S), :] = at_slots[k][0:S]
    block[pl.ds(SIDX, S), :] = slot_place.astype(f32)[0:S]
    block[pl.ds(SIDX + S, ROWS - SIDX - S), :] = jnp.zeros((ROWS - SIDX - S, 128), f32)

    for k in range(9):
        for r in range(8):
            water[k, pl.ds(r, 1)] = wpos[pl.ds(k, 1), pl.ds(128 * r, 128)]
            water[9 + k, pl.ds(r, 1)] = wvel[pl.ds(k, 1), pl.ds(128 * r, 128)]
    new = settle([water[k] for k in range(9)], [water[9 + k] for k in range(9)])
    for k in range(9):
        water[k] = new[k]
        for r in range(8):
            wout[pl.ds(k, 1), pl.ds(128 * r, 128)] = water[k, pl.ds(r, 1)]


def pick(tables, rows, lanes):
    outs = [[] for _ in tables]
    for row_at, lane_at in zip(rows, lanes):
        hits = [row_at == r for r in range(len(tables[0]))]
        for out, table in zip(outs, tables):
            acc = jnp.zeros((8, 128), f32)
            for hit, part in zip(hits, table):
                acc = jnp.where(hit, take(part, lane_at), acc)
            out.append(acc)
    return outs


def swap(slots):
    back = [pltpu.roll(part, 7, 0) for part in slots[3:6]]
    ahead = [pltpu.roll(part, 1, 0) for part in slots[0:3]]
    return back + ahead


def rounds(
    data, local, vel, out,
    w, g, m, prow, plane, crow, clane, cont, pf, pb, x, xt, wc, d, length, scale, delta,
    sw, sm, srow, slane, sww, sx, sxt, sd, slength, sscale, sdelta,
):
    def rows_at(base, count):
        return [data[:, base + r, :] for r in range(count)]

    for base, row_ref, lane_ref, count in ((PIDX, prow, plane, E), (CIDX, crow, clane, E), (SIDX, srow, slane, S)):
        for r in range(count):
            value = data[:, base + r, :].astype(i32)
            row_ref[r] = value >> 7
            lane_ref[r] = value & 127
    keep = rows_at(CONT, E)
    run = jnp.ones((8, 128), f32)
    for r in range(E):
        cont[r] = keep[r]
        if r > 0:
            run = run * keep[r]
        pf[r] = run
    whole = run
    run = jnp.ones((8, 128), f32)
    for r in range(E - 1, -1, -1):
        pb[r] = run
        run = run * keep[r]
    extra = jnp.max(jnp.sum(whole, axis=1, keepdims=True)).astype(i32)
    opens = keep[0]
    closes = pltpu.roll(opens, 127, 1)

    def geometry(diff, dvel, s):
        far = jnp.sqrt(dot3(diff, diff))
        ratio = s / far
        weight = [ratio * part for part in diff]
        moved = [diff[k] + time_step * dvel[k] for k in range(3)]
        return far, weight, moved, time_step * dot3(weight, dvel)

    own = [rows_at(SPOS + S * k, S) for k in range(7)]
    twin = [swap(part) for part in own]
    for r in range(S):
        diff = [own[k][r] - twin[k][r] for k in range(3)]
        dvel = [own[3 + k][r] - twin[3 + k][r] for k in range(3)]
        s = 1.0 / jnp.sqrt(own[6][r] + twin[6][r])
        far, weight, moved, first = geometry(diff, dvel, s)
        for k in range(3):
            sw[k, r] = weight[k]
            sd[k, r] = moved[k]
            sdelta[k, r] = jnp.zeros((8, 128), f32)
        sm[r] = own[6][r]
        sww[r] = dot3(weight, weight)
        slength[r] = far
        sscale[r] = s
        sx[r] = first
    near = pick(
        [[sw[k, r] for r in range(S)] for k in range(3)],
        [crow[r] for r in range(E)],
        [clane[r] for r in range(E)],
    )
    for r in range(E):
        diff = [data[:, DIFF + E * k + r, :] for k in range(3)]
        dvel = [data[:, DVEL + E * k + r, :] for k in range(3)]
        s = data[:, SCALE + r, :]
        far, weight, moved, first = geometry(diff, dvel, s)
        for k in range(3):
            w[k, r] = weight[k]
            d[k, r] = moved[k]
            wc[k, r] = near[k][r]
            delta[k, r] = jnp.zeros((8, 128), f32)
        g[r] = dot3(weight, [near[k][r] for k in range(3)])
        m[r] = data[:, MASS + r, :]
        length[r] = far
        scale[r] = s
        x[r] = first

    def totals(parts):
        count = len(parts)
        inside = []
        for part in parts:
            acc = part[0]
            fwd = [acc]
            for r in range(1, E):
                acc = part[r] + cont[r] * acc
                fwd.append(acc)
            for r in range(E - 2, -1, -1):
                fwd[r] = jnp.where(cont[r + 1] > 0.0, fwd[r + 1], fwd[r])
            inside.append(fwd)
        ahead = tuple(opens * pltpu.roll(part[E - 1], 1, 1) for part in inside)
        back = tuple(closes * pltpu.roll(part[0], 127, 1) for part in inside)

        def spread(_, now):
            ahead_now, back_now = now[:count], now[count:]
            new = [ahead[k] + opens * pltpu.roll(whole * ahead_now[k], 1, 1) for k in range(count)]
            new += [back[k] + closes * pltpu.roll(whole * back_now[k], 127, 1) for k in range(count)]
            return tuple(new)

        carried = lax.fori_loop(0, extra, spread, ahead + back)
        return [
            [
                inside[k][r] + pf[r] * carried[k] + pb[r] * carried[count + k]
                for r in range(E)
            ]
            for k in range(count)
        ]

    def apply_k(_, carry):
        sums = totals(
            [[w[k, r] * x[r] for r in range(E)] for k in range(3)]
            + [[g[r] * x[r] for r in range(E)]]
        )
        slot_x = [sx[r] for r in range(S)]
        cross_x = pick([slot_x], [crow[r] for r in range(E)], [clane[r] for r in range(E)])[0]
        slot_sum = pick([sums[3]], [srow[r] for r in range(S)], [slane[r] for r in range(S)])[0]
        z = [
            m[r] * (w[0, r] * sums[0][r] + w[1, r] * sums[1][r] + w[2, r] * sums[2][r] + g[r] * cross_x[r])
            for r in range(E)
        ]
        slot_z = [sm[r] * (slot_sum[r] + sww[r] * slot_x[r]) for r in range(S)]
        slot_twin = swap(slot_z)
        for r in range(S):
            new = slot_x[r] - (slot_z[r] + slot_twin[r])
            sx[r] = new
            sxt[r] = sxt[r] + new
        z_twin = pick([z], [prow[r] for r in range(E)], [plane[r] for r in range(E)])[0]
        for r in range(E):
            new = x[r] - (z[r] + z_twin[r])
            x[r] = new
            xt[r] = xt[r] + new
        return carry

    def solve(index, carry):
        for r in range(E):
            xt[r] = x[r]
        for r in range(S):
            sxt[r] = sx[r]
        lax.fori_loop(0, ORDER, apply_k, 0)
        sums = totals([[w[k, r] * xt[r] for r in range(E)] for k in range(3)])
        slot_xt = [sxt[r] for r in range(S)]
        cross_x = pick([slot_xt], [crow[r] for r in range(E)], [clane[r] for r in range(E)])[0]
        slot_sum = pick(sums, [srow[r] for r in range(S)], [slane[r] for r in range(S)])
        for k in range(3):
            for r in range(E):
                delta[k, r] = delta[k, r] - m[r] * (sums[k][r] + wc[k, r] * cross_x[r])
            for r in range(S):
                sdelta[k, r] = sdelta[k, r] - sm[r] * (slot_sum[k][r] + sw[k, r] * slot_xt[r])

        @pl.when(index < ITER)
        def _():
            def lengthening(gap, far, s):
                target = jnp.sqrt(2.0 * far * far - dot3(gap, gap))
                return s * (far - target)

            here = [[delta[k, r] for r in range(E)] for k in range(3)]
            there = pick(here, [prow[r] for r in range(E)], [plane[r] for r in range(E)])
            for r in range(E):
                gap = [d[k, r] + (here[k][r] - there[k][r]) for k in range(3)]
                x[r] = lengthening(gap, length[r], scale[r])
            here = [[sdelta[k, r] for r in range(S)] for k in range(3)]
            there = [swap(part) for part in here]
            for r in range(S):
                gap = [sd[k, r] + (here[k][r] - there[k][r]) for k in range(3)]
                sx[r] = lengthening(gap, slength[r], sscale[r])

        return carry

    lax.fori_loop(0, ITER + 1, solve, 0)

    me = lax.axis_index("dom")

    def own_row(ref, k):
        return lambda r: jnp.broadcast_to(ref[k, r, pl.ds(me, 1), :], (8, 128))

    places = [local[pl.ds(8 * q, 8), :].astype(i32) for q in range(4)]
    rows, lanes = [p >> 7 for p in places], [p & 127 for p in places]
    inner = gather_rows([own_row(delta, k) for k in range(3)], E, rows[:2], lanes[:2])
    outer = gather_rows([own_row(sdelta, k) for k in range(3)], S, rows[2:], lanes[2:])
    for q in range(2):
        for k in range(3):
            xt[3 * q + k] = jnp.where(rows[q] >= 0, inner[q][k], outer[q][k])
    for k in range(3):
        for r in range(16):
            at = pl.ds(128 * r, 128)
            change = xt[3 * (r // 8) + k, pl.ds(r % 8, 1), :]
            out[pl.ds(k, 1), at] = vel[pl.ds(k, 1), at] + change / time_step


def on_device(
    protein_pos, protein_vel, inv_mass, bond_atoms, left_atoms, right_atoms, water_pos, water_vel
):
    vmem = pl.BlockSpec(memory_space=pltpu.VMEM)
    block, local, water_velocity = pl.pallas_call(
        prepare,
        out_shape=(
            jax.ShapeDtypeStruct((ROWS, 128), f32),
            jax.ShapeDtypeStruct((32, 128), f32),
            jax.ShapeDtypeStruct(water_pos.shape, f32),
        ),
        in_specs=[vmem] * 8,
        out_specs=(vmem,) * 3,
        scratch_shapes=[
            pltpu.VMEM((7, 16, 128), f32),
            pltpu.VMEM((32, 128), i32),
            pltpu.VMEM((24, 128), i32),
            pltpu.VMEM((24, 128), i32),
            pltpu.VMEM((32, 128), i32),
            pltpu.VMEM((8, 128), i32),
            pltpu.VMEM((18, 8, 128), f32),
        ],
        name="prepare",
    )(
        protein_pos,
        protein_vel,
        inv_mass.reshape(16, 128),
        bond_atoms,
        left_atoms.reshape(3, 128),
        right_atoms.reshape(3, 128),
        water_pos,
        water_vel,
    )
    data = lax.all_gather(block, "dom")
    real = [(3, E), (E,), (E,)]
    scratch = [
        ((3, E), f32), ((E,), f32), ((E,), f32),
        ((E,), i32), ((E,), i32), ((E,), i32), ((E,), i32),
        ((E,), f32), ((E,), f32), ((E,), f32),
        ((E,), f32), ((E,), f32),
        ((3, E), f32), ((3, E), f32), ((E,), f32), ((E,), f32), ((3, E), f32),
        ((3, S), f32), ((S,), f32), ((S,), i32), ((S,), i32), ((S,), f32),
        ((S,), f32), ((S,), f32), ((3, S), f32), ((S,), f32), ((S,), f32), ((3, S), f32),
    ]
    protein_velocity = pl.pallas_call(
        rounds,
        out_shape=jax.ShapeDtypeStruct(protein_vel.shape, f32),
        in_specs=[vmem] * 3,
        out_specs=vmem,
        scratch_shapes=[pltpu.VMEM(shape + (8, 128), kind) for shape, kind in scratch],
        name="rounds",
    )(data, local, protein_vel)
    return (protein_velocity, water_velocity)


def solution(mesh):
    in_specs = (
        P(None, ("rep", "dom")),
        P(None, ("rep", "dom")),
        P(("rep", "dom")),
        P(None, ("rep", "dom")),
        P(("rep", "dom")),
        P(("rep", "dom")),
        P(None, ("rep", "dom")),
        P(None, ("rep", "dom")),
    )
    out_specs = (P(None, ("rep", "dom")), P(None, ("rep", "dom")))
    return jax.shard_map(
        on_device, mesh=mesh, in_specs=in_specs, out_specs=out_specs, check_vma=False
    )
```

time: 801 us -> 81.6 us (0.10)
  the two profiles are of different devices: /device:TPU:1 before, /device:TPU:2 now
where the time goes in v1:
time: 81.6 us; the launch traced here: 81.4 us
  waiting for transfers between devices  40.4 us (50%)
  Pallas kernels  27 us (33%)
  between operations  14 us (17%)
    all_gather x1, waiting for transfers between devices, on_device(): data = lax.all_gather(block, 'dom')  40.4 us
    pallas_call x1, Pallas kernels, on_device(): pl.pallas_call(rounds, out_shape=jax.ShapeDtypeStruct(protein_vel.shape,...  21.5 us
    pallas_call x1, Pallas kernels, on_device(): pl.pallas_call(prepare, out_shape=(jax.ShapeDtypeStruct((ROWS, 128), f32)...  5.53 us
  transfers between devices with their start and end apart: 1, of which 1 were waited for; matrix products, arithmetic and copies ran while one was open for 0% of the time, Pallas kernels for 0%

profile of v1, /device:TPU:2, one launch (start us, length us, event | category | flops | bytes accessed | tf_op | source)
XLA Modules:
  0.0 81.4 jit_solution(9198378869859260491)
XLA Ops:
  7.2 0.0 all-gather.3.cloned.1.call-start
  7.2 5.5 %prepare.1 = (f32[272,128]{1,0:T(8,128)}, f32[32,128]{1,0:T(8,128)}, f32[9,1024]{1,0:T(8,128)}) custom-call(f32[3,2048]{1,0:T(4,128)} %pos.1, f32[3,2048]{1,0:T(4,128)} %vel.3, f32[16,128]{1,0:T(8,128)} %bitcast.5, s32[2,1280]{1,0:T(2,128)} %bonds.1, s32[3,128]{1,0:T(4,128)} %bitcast.6, s32[3,128]{1,0:T(4,128)} %bitcast.7, f32[9,1024]{1,0:T(8,128)} %wpos.1, ...), custom_call_target="tpu_custom_call" | custom-call | tf_op jit(solution)/shard_map/prepare/pallas_call | solution.py:509
  12.7 0.0 all-gather.3.cloned.1.call-update
  12.8 40.4 %all-gather.3.cloned.1.call-done = f32[2176,128]{1,0:T(8,128)} async-done(((f32[272,128]{1,0:T(8,128)}), f32[2176,128]{1,0:T(8,128)}) %all-gather.3.cloned.1.call-update) | async-done | bytes 1114128 | tf_op jit(solution)/shard_map/all_gather | solution.py:538
  53.1 21.5 %rounds.1 = f32[3,2048]{1,0:T(4,128)} custom-call(f32[8,272,128]{2,1,0:T(8,128)} %bitcast.4, f32[32,128]{1,0:T(8,128)} %get-tuple-element.6.local, f32[3,2048]{1,0:T(4,128)} %vel.3), custom_call_target="tpu_custom_call" | custom-call | tf_op jit(solution)/shard_map/rounds/pallas_call | solution.py:549
Async XLA Ops:
  7.2 45.9 %all-gather.3.cloned.1.call-start = ((), (), s32[]{:S(2)}) async-start(), calls=%async_computation | async-start | bytes 1253376 | tf_op jit(solution)/shard_map/all_gather | solution.py:538
Sparse Core Ops, SparseCore 0:
  12.9 40.1 all-gather.2

commit v2 on v1

--- a/solution.py
+++ b/solution.py
@@ -502,6 +502,90 @@
             out[pl.ds(k, 1), at] = vel[pl.ds(k, 1), at] + change / time_step
 
 
+CHUNKS = ((0, 72), (72, 72), (144, 64), (208, 64))
+
+
+def share(block, out, send, recv, local_sem):
+    me = lax.axis_index("dom")
+    count = out.shape[0]
+    last = count // 2 - 1
+    z, core = me // 2, me % 2
+    partner, up, down = 2 * z + 1 - core, me + 2, me - 2
+
+    barrier = pltpu.get_barrier_semaphore()
+
+    def greet(target):
+        pl.semaphore_signal(
+            barrier, inc=1, device_id={"dom": target}, device_id_type=pl.DeviceIdType.MESH
+        )
+
+    greet(partner)
+
+    @pl.when(z < last)
+    def _():
+        greet(up)
+
+    @pl.when(z > 0)
+    def _():
+        greet(down)
+
+    peers = 1 + jnp.where(z < last, 1, 0) + jnp.where(z > 0, 1, 0)
+    pl.semaphore_wait(barrier, peers)
+
+    def copy(origin, source, k, target, sem):
+        rows = pl.ds(*CHUNKS[k])
+        return pltpu.make_async_remote_copy(
+            src_ref=origin.at[rows],
+            dst_ref=out.at[source, rows],
+            send_sem=send.at[sem, k],
+            recv_sem=recv.at[source, k],
+            device_id={"dom": target},
+            device_id_type=pl.DeviceIdType.MESH,
+        )
+
+    here = pltpu.make_async_copy(block, out.at[me], local_sem)
+    here.start()
+    sent = []
+
+    def push(when, origin, source, k, target, sem):
+        sent.append((when, origin, source, k, target, sem))
+
+        @pl.when(when)
+        def _():
+            copy(origin, source, k, target, sem).start()
+
+    for k in range(len(CHUNKS)):
+        push(z < last, block, me, k, up, 0)
+        push(z > 0, block, me, k, down, 1)
+        push(z >= 0, block, me, k, partner, 2)
+    for away in range(1, last + 1):
+        for k in range(len(CHUNKS)):
+            for side, arrives, source, onward, target in (
+                (0, z >= away, me - 2 * away, z < last, up),
+                (1, z + away <= last, me + 2 * away, z > 0, down),
+            ):
+                sem = 3 + 4 * (away - 1) + 2 * side
+
+                @pl.when(arrives)
+                def _(source=source, k=k):
+                    copy(out.at[source], source, k, partner, 0).wait_recv()
+
+                if away < last:
+                    push(arrives & onward, out.at[source], source, k, target, sem)
+                push(arrives, out.at[source], source, k, partner, sem + 1)
+    for k in range(len(CHUNKS)):
+        for chip in range(last + 1):
+            source = 2 * chip + 1 - core
+            copy(out.at[source], source, k, partner, 0).wait_recv()
+    for when, origin, source, k, target, sem in sent:
+
+        @pl.when(when)
+        def _(origin=origin, source=source, k=k, target=target, sem=sem):
+            copy(origin, source, k, target, sem).wait_send()
+
+    here.wait()
+
+
 def on_device(
     protein_pos, protein_vel, inv_mass, bond_atoms, left_atoms, right_atoms, water_pos, water_vel
 ):
@@ -535,7 +619,20 @@
         water_pos,
         water_vel,
     )
-    data = lax.all_gather(block, "dom")
+    count = lax.axis_size("dom")
+    data = pl.pallas_call(
+        share,
+        out_shape=jax.ShapeDtypeStruct((count, ROWS, 128), f32),
+        in_specs=[vmem],
+        out_specs=vmem,
+        scratch_shapes=[
+            pltpu.SemaphoreType.DMA((4 * count // 2, len(CHUNKS))),
+            pltpu.SemaphoreType.DMA((count, len(CHUNKS))),
+            pltpu.SemaphoreType.DMA,
+        ],
+        compiler_params=pltpu.CompilerParams(collective_id=0, has_side_effects=True),
+        name="share",
+    )(block)
     real = [(3, E), (E,), (E,)]
     scratch = [
         ((3, E), f32), ((E,), f32), ((E,), f32),

time: 81.6 us -> 47 us (0.58)
  the two profiles are of different devices: /device:TPU:2 before, /device:TPU:1 now
where the time goes in v2:
time: 47 us; the launch traced here: 46.8 us
  Pallas kernels  46.2 us (98%)
  between operations  0.64 us (1%)
    pallas_call x1, Pallas kernels, on_device(): pl.pallas_call(rounds, out_shape=jax.ShapeDtypeStruct(protein_vel.shape,...  21.5 us
    pallas_call x1, Pallas kernels, on_device(): pl.pallas_call(share, out_shape=jax.ShapeDtypeStruct((count, ROWS, 128),...  19.2 us
    pallas_call x1, Pallas kernels, on_device(): pl.pallas_call(prepare, out_shape=(jax.ShapeDtypeStruct((ROWS, 128), f32)...  5.53 us

profile of v2, /device:TPU:1, one launch (start us, length us, event | category | flops | bytes accessed | tf_op | source)
XLA Modules:
  0.0 46.8 jit_solution(14843362588315851881)
XLA Ops:
  0.6 5.5 %prepare.1 = (f32[272,128]{1,0:T(8,128)}, f32[32,128]{1,0:T(8,128)}, f32[9,1024]{1,0:T(8,128)}) custom-call(f32[3,2048]{1,0:T(4,128)} %pos.1, f32[3,2048]{1,0:T(4,128)} %vel.3, f32[16,128]{1,0:T(8,128)} %bitcast.3, s32[2,1280]{1,0:T(2,128)} %bonds.1, s32[3,128]{1,0:T(4,128)} %bitcast.4, s32[3,128]{1,0:T(4,128)} %bitcast.5, f32[9,1024]{1,0:T(8,128)} %wpos.1, ...), custom_call_target="tpu_custom_call" | custom-call | tf_op jit(solution)/shard_map/prepare/pallas_call | solution.py:593
  6.2 19.2 %share.1.data = f32[8,272,128]{2,1,0:T(8,128)} custom-call(f32[272,128]{1,0:T(8,128)} %get-tuple-element.5.block), custom_call_target="tpu_custom_call" | custom-call | tf_op jit(solution)/shard_map/share/pallas_call | solution.py:623
  25.4 21.5 %rounds.1 = f32[3,2048]{1,0:T(4,128)} custom-call(f32[8,272,128]{2,1,0:T(8,128)} %share.1.data, f32[32,128]{1,0:T(8,128)} %get-tuple-element.6.local, f32[3,2048]{1,0:T(4,128)} %vel.3), custom_call_target="tpu_custom_call" | custom-call | tf_op jit(solution)/shard_map/rounds/pallas_call | solution.py:646

commit v3 on v2

--- a/solution.py
+++ b/solution.py
@@ -169,8 +169,7 @@
 
 
 def prepare(
-    pos, vel, mass, bonds, left, right, wpos, wvel, block, local, wout,
-    table, ends, keys, atoms, before, slots, water,
+    pos, vel, mass, bonds, left, right, block, local, table, ends, keys, atoms, before, slots,
 ):
     lane = lax.broadcasted_iota(i32, (8, 128), 1)
     sub = lax.broadcasted_iota(i32, (8, 128), 0)
@@ -289,6 +288,8 @@
     block[pl.ds(SIDX, S), :] = slot_place.astype(f32)[0:S]
     block[pl.ds(SIDX + S, ROWS - SIDX - S), :] = jnp.zeros((ROWS - SIDX - S, 128), f32)
 
+
+def waters(wpos, wvel, wout, water):
     for k in range(9):
         for r in range(8):
             water[k, pl.ds(r, 1)] = wpos[pl.ds(k, 1), pl.ds(128 * r, 128)]
@@ -319,10 +320,15 @@
 
 
 def rounds(
-    data, local, vel, out,
+    data, local, vel_in, water, out, water_out,
     w, g, m, prow, plane, crow, clane, cont, pf, pb, x, xt, wc, d, length, scale, delta,
-    sw, sm, srow, slane, sww, sx, sxt, sd, slength, sscale, sdelta,
+    sw, sm, srow, slane, sww, sx, sxt, sd, slength, sscale, sdelta, vel, vel_sem, water_sem,
 ):
+    load = pltpu.make_async_copy(vel_in, vel, vel_sem)
+    load.start()
+    passed = pltpu.make_async_copy(water, water_out, water_sem)
+    passed.start()
+
     def rows_at(base, count):
         return [data[:, base + r, :] for r in range(count)]
 
@@ -488,6 +494,7 @@
     def own_row(ref, k):
         return lambda r: jnp.broadcast_to(ref[k, r, pl.ds(me, 1), :], (8, 128))
 
+    load.wait()
     places = [local[pl.ds(8 * q, 8), :].astype(i32) for q in range(4)]
     rows, lanes = [p >> 7 for p in places], [p & 127 for p in places]
     inner = gather_rows([own_row(delta, k) for k in range(3)], E, rows[:2], lanes[:2])
@@ -500,18 +507,34 @@
             at = pl.ds(128 * r, 128)
             change = xt[3 * (r // 8) + k, pl.ds(r % 8, 1), :]
             out[pl.ds(k, 1), at] = vel[pl.ds(k, 1), at] + change / time_step
+    passed.wait()
 
 
 CHUNKS = ((0, 72), (72, 72), (144, 64), (208, 64))
 
 
-def share(block, out, send, recv, local_sem):
+def share(
+    pos_in, vel_in, mass_in, bonds_in, left_in, right_in, wpos_in, wvel_in, out, local, wout,
+    pos, vel, mass, bonds, left, right, wpos, wvel,
+    block, table, ends, keys, atoms, before, slots, water, send, recv, local_sem, load_sem,
+):
     me = lax.axis_index("dom")
     count = out.shape[0]
     last = count // 2 - 1
     z, core = me // 2, me % 2
     partner, up, down = 2 * z + 1 - core, me + 2, me - 2
 
+    loads = [
+        pltpu.make_async_copy(origin, target, load_sem.at[k])
+        for k, (origin, target) in enumerate(
+            (
+                (bonds_in, bonds), (pos_in, pos), (vel_in, vel), (mass_in, mass),
+                (left_in, left), (right_in, right), (wpos_in, wpos), (wvel_in, wvel),
+            )
+        )
+    ]
+    for load in loads:
+        load.start()
     barrier = pltpu.get_barrier_semaphore()
 
     def greet(target):
@@ -530,6 +553,11 @@
         greet(down)
 
     peers = 1 + jnp.where(z < last, 1, 0) + jnp.where(z > 0, 1, 0)
+    for load in loads[:6]:
+        load.wait()
+    prepare(
+        pos, vel, mass, bonds, left, right, block, local, table, ends, keys, atoms, before, slots
+    )
     pl.semaphore_wait(barrier, peers)
 
     def copy(origin, source, k, target, sem):
@@ -558,6 +586,9 @@
         push(z < last, block, me, k, up, 0)
         push(z > 0, block, me, k, down, 1)
         push(z >= 0, block, me, k, partner, 2)
+    for load in loads[6:]:
+        load.wait()
+    waters(wpos, wvel, wout, water)
     for away in range(1, last + 1):
         for k in range(len(CHUNKS)):
             for side, arrives, source, onward, target in (
@@ -590,16 +621,27 @@
     protein_pos, protein_vel, inv_mass, bond_atoms, left_atoms, right_atoms, water_pos, water_vel
 ):
     vmem = pl.BlockSpec(memory_space=pltpu.VMEM)
-    block, local, water_velocity = pl.pallas_call(
-        prepare,
+    hbm = pl.BlockSpec(memory_space=pltpu.HBM)
+    count = lax.axis_size("dom")
+    data, local, water_velocity = pl.pallas_call(
+        share,
         out_shape=(
-            jax.ShapeDtypeStruct((ROWS, 128), f32),
+            jax.ShapeDtypeStruct((count, ROWS, 128), f32),
             jax.ShapeDtypeStruct((32, 128), f32),
             jax.ShapeDtypeStruct(water_pos.shape, f32),
         ),
-        in_specs=[vmem] * 8,
+        in_specs=[hbm] * 8,
         out_specs=(vmem,) * 3,
         scratch_shapes=[
+            pltpu.VMEM(protein_pos.shape, f32),
+            pltpu.VMEM(protein_vel.shape, f32),
+            pltpu.VMEM((16, 128), f32),
+            pltpu.VMEM(bond_atoms.shape, i32),
+            pltpu.VMEM((3, 128), i32),
+            pltpu.VMEM((3, 128), i32),
+            pltpu.VMEM(water_pos.shape, f32),
+            pltpu.VMEM(water_vel.shape, f32),
+            pltpu.VMEM((ROWS, 128), f32),
             pltpu.VMEM((7, 16, 128), f32),
             pltpu.VMEM((32, 128), i32),
             pltpu.VMEM((24, 128), i32),
@@ -607,33 +649,30 @@
             pltpu.VMEM((32, 128), i32),
             pltpu.VMEM((8, 128), i32),
             pltpu.VMEM((18, 8, 128), f32),
-        ],
-        name="prepare",
-    )(
-        protein_pos,
-        protein_vel,
-        inv_mass.reshape(16, 128),
-        bond_atoms,
-        left_atoms.reshape(3, 128),
-        right_atoms.reshape(3, 128),
-        water_pos,
-        water_vel,
-    )
-    count = lax.axis_size("dom")
-    data = pl.pallas_call(
-        share,
-        out_shape=jax.ShapeDtypeStruct((count, ROWS, 128), f32),
-        in_specs=[vmem],
-        out_specs=vmem,
-        scratch_shapes=[
             pltpu.SemaphoreType.DMA((4 * count // 2, len(CHUNKS))),
             pltpu.SemaphoreType.DMA((count, len(CHUNKS))),
             pltpu.SemaphoreType.DMA,
+            pltpu.SemaphoreType.DMA((8,)),
         ],
-        compiler_params=pltpu.CompilerParams(collective_id=0, has_side_effects=True),
+        compiler_params=pltpu.CompilerParams(
+            collective_id=0, has_side_effects=True, vmem_limit_bytes=16 * 2**20
+        ),
         name="share",
-    )(block)
-    real = [(3, E), (E,), (E,)]
+    )(
+        *(
+            pltpu.with_memory_space_constraint(value, pltpu.HBM)
+            for value in (
+                protein_pos,
+                protein_vel,
+                inv_mass.reshape(16, 128),
+                bond_atoms,
+                left_atoms.reshape(3, 128),
+                right_atoms.reshape(3, 128),
+                water_pos,
+                water_vel,
+            )
+        )
+    )
     scratch = [
         ((3, E), f32), ((E,), f32), ((E,), f32),
         ((E,), i32), ((E,), i32), ((E,), i32), ((E,), i32),
@@ -643,14 +682,19 @@
         ((3, S), f32), ((S,), f32), ((S,), i32), ((S,), i32), ((S,), f32),
         ((S,), f32), ((S,), f32), ((3, S), f32), ((S,), f32), ((S,), f32), ((3, S), f32),
     ]
-    protein_velocity = pl.pallas_call(
+    protein_velocity, water_velocity = pl.pallas_call(
         rounds,
-        out_shape=jax.ShapeDtypeStruct(protein_vel.shape, f32),
-        in_specs=[vmem] * 3,
-        out_specs=vmem,
-        scratch_shapes=[pltpu.VMEM(shape + (8, 128), kind) for shape, kind in scratch],
+        out_shape=(
+            jax.ShapeDtypeStruct(protein_vel.shape, f32),
+            jax.ShapeDtypeStruct(water_vel.shape, f32),
+        ),
+        in_specs=[vmem, vmem, hbm, vmem],
+        out_specs=(vmem, hbm),
+        scratch_shapes=[pltpu.VMEM(shape + (8, 128), kind) for shape, kind in scratch]
+        + [pltpu.VMEM(protein_vel.shape, f32), pltpu.SemaphoreType.DMA, pltpu.SemaphoreType.DMA],
+        compiler_params=pltpu.CompilerParams(vmem_limit_bytes=16 * 2**20),
         name="rounds",
-    )(data, local, protein_vel)
+    )(data, local, pltpu.with_memory_space_constraint(protein_vel, pltpu.HBM), water_velocity)
     return (protein_velocity, water_velocity)
 
 

time: 47 us -> 42.5 us (0.904)
  Pallas kernels: 46.2 us -> 41.7 us
    pallas_call x3 -> x2, Pallas kernels: 46.2 us -> 41.7 us  [the longest x1 21.4 us: on_device(): pl.pallas_call(share, out_shape=(jax.ShapeDtypeStruct((count, ROWS, 128),...]
where the time goes in v3:
time: 42.5 us; the launch traced here: 42.4 us
  Pallas kernels  41.7 us (98%)
  between operations  0.64 us (2%)
    pallas_call x1, Pallas kernels, on_device(): pl.pallas_call(share, out_shape=(jax.ShapeDtypeStruct((count, ROWS, 128),...  21.4 us
    pallas_call x1, Pallas kernels, on_device(): pl.pallas_call(rounds, out_shape=(jax.ShapeDtypeStruct(protein_vel.shape,...  20.3 us

profile of v3, /device:TPU:1, one launch (start us, length us, event | category | flops | bytes accessed | tf_op | source)
XLA Modules:
  0.0 42.4 jit_solution(10061270840474528333)
XLA Ops:
  0.6 21.4 %share.1 = (f32[8,272,128]{2,1,0:T(8,128)S(1)}, f32[32,128]{1,0:T(8,128)S(1)}, f32[9,1024]{1,0:T(8,128)S(1)}) custom-call(f32[3,2048]{1,0:T(4,128)} %pos_in.1, f32[3,2048]{1,0:T(4,128)} %vel_in.3, f32[16,128]{1,0:T(8,128)} %bitcast.3, s32[2,1280]{1,0:T(2,128)} %bonds_in.1, s32[3,128]{1,0:T(4,128)} %bitcast.4, s32[3,128]{1,0:T(4,128)} %bitcast.5, ...), custom_call_target="tpu_custom_call" | custom-call | tf_op jit(solution)/shard_map/share/pallas_call | solution.py:626
  22.1 20.3 %rounds.1 = (f32[3,2048]{1,0:T(4,128)}, f32[9,1024]{1,0:T(8,128)}) custom-call(f32[8,272,128]{2,1,0:T(8,128)S(1)} %get-tuple-element.5.data, f32[32,128]{1,0:T(8,128)S(1)} %get-tuple-element.6.local, f32[3,2048]{1,0:T(4,128)} %vel_in.3, f32[9,1024]{1,0:T(8,128)S(1)} %get-tuple-element.7.water), custom_call_target="tpu_custom_call" | custom-call | tf_op jit(solution)/shard_map/rounds/pallas_call | solution.py:685

commit v4 on v3

--- a/solution.py
+++ b/solution.py
@@ -21,12 +21,15 @@
 oxygen_reach = 2.0 * mass_hydrogen * water_height / total_mass
 hydrogen_reach = water_height - oxygen_reach
 
+B = 10
+S = 6
+DIFF, DVEL, SCALE, SPOS = 0, 3 * B, 6 * B, 7 * B
+SVEL, SMASS = SPOS + 3 * S, SPOS + 6 * S
+EARLY = SPOS + 7 * S
 E = 20
-S = 6
-DIFF, DVEL, SCALE, MASS, PIDX, CONT, CIDX = 0, 3 * E, 6 * E, 7 * E, 8 * E, 9 * E, 10 * E
-SPOS = 11 * E
-SVEL, SMASS, SIDX = SPOS + 3 * S, SPOS + 6 * S, SPOS + 7 * S
-ROWS = 272
+MASS, PIDX, CONT, CIDX, HIDX = EARLY, EARLY + E, EARLY + 2 * E, EARLY + 3 * E, EARLY + 4 * E
+SIDX = EARLY + 5 * E
+ROWS = 224
 f32, i32 = jnp.float32, jnp.int32
 
 
@@ -168,11 +171,7 @@
     return read
 
 
-def prepare(
-    pos, vel, mass, bonds, left, right, block, local, table, ends, keys, atoms, before, slots,
-):
-    lane = lax.broadcasted_iota(i32, (8, 128), 1)
-    sub = lax.broadcasted_iota(i32, (8, 128), 0)
+def bonds_as_given(pos, vel, mass, bonds, left, right, block, table, ends, slots):
     for r in range(16):
         at = pl.ds(128 * r, 128)
         for k in range(3):
@@ -188,6 +187,26 @@
         slots[pl.ds(r, 1), :] = right[pl.ds(r, 1), :]
         slots[pl.ds(3 + r, 1), :] = left[pl.ds(r, 1), :]
 
+    tables = [row_of(table, k) for k in range(7)]
+    atoms = [ends[pl.ds(8 * q, 8), :] for q in range(4)] + [slots[...]]
+    at = gather_rows(tables, 16, [a >> 7 for a in atoms], [a & 127 for a in atoms])
+    for q in range(2):
+        size = min(8, B - 8 * q)
+
+        def put(base, value):
+            block[pl.ds(base + 8 * q, size), :] = value[0:size]
+
+        for k in range(3):
+            put(DIFF + B * k, at[q][k] - at[2 + q][k])
+            put(DVEL + B * k, at[q][3 + k] - at[2 + q][3 + k])
+        put(SCALE, 1.0 / jnp.sqrt(at[q][6] + at[2 + q][6]))
+    for k in range(7):
+        block[pl.ds(SPOS + S * k, S), :] = at[4][k][0:S]
+
+
+def order_bonds(ends, before):
+    lane = lax.broadcasted_iota(i32, (8, 128), 1)
+    sub = lax.broadcasted_iota(i32, (8, 128), 0)
     start = []
     for q in range(4):
         at = sub + 8 * q
@@ -195,6 +214,11 @@
     done = sort4(start)
     for q in range(4):
         before[pl.ds(8 * q, 8), :] = done[q]
+
+
+def use_order(block, local, table, ends, keys, atoms, before, slots):
+    lane = lax.broadcasted_iota(i32, (8, 128), 1)
+    sub = lax.broadcasted_iota(i32, (8, 128), 0)
     rows, lanes = [], []
     for q in range(3):
         n = jnp.minimum(lane * E + sub + 8 * q, 4095)
@@ -262,29 +286,21 @@
     before[pl.ds(0, 1), :] = pltpu.roll(atoms[pl.ds(E - 1, 1), :], 1, 1)
     before[pl.ds(1, E - 1), :] = atoms[pl.ds(0, E - 1), :]
     own_rows, own_lanes = [a >> 7 for a in atom], [a & 127 for a in atom]
-    tables = [row_of(table, k) for k in range(7)] + [row_of(local.at[pl.ds(16, 16)])]
-    own = gather_rows(tables, 16, own_rows, own_lanes)
-    far = gather_rows(tables[:7], 16, [a >> 7 for a in other], [a & 127 for a in other])
+    own = gather_rows([row_of(table, 6), row_of(local.at[pl.ds(16, 16)])], 16, own_rows, own_lanes)
     for q in range(3):
         size = min(8, E - 8 * q)
 
         def put(base, value):
             block[pl.ds(base + 8 * q, size), :] = value[0:size]
 
-        for k in range(3):
-            put(DIFF + E * k, own[q][k] - far[q][k])
-            put(DVEL + E * k, own[q][3 + k] - far[q][3 + k])
-        put(SCALE, 1.0 / jnp.sqrt(own[q][6] + far[q][6]))
-        put(MASS, own[q][6])
+        put(MASS, own[q][0])
         put(PIDX, places[q].astype(f32))
         same = before[pl.ds(8 * q, 8), :] == atom[q]
         if q == 0:
             same = same & ((lane > 0) | (sub > 0))
         put(CONT, jnp.where(same, 1.0, 0.0))
-        put(CIDX, own[q][7])
-    at_slots = gather_rows(tables[:7], 16, [slot_atom >> 7], [slot_atom & 127])[0]
-    for k in range(7):
-        block[pl.ds(SPOS + S * k, S), :] = at_slots[k][0:S]
+        put(CIDX, own[q][1])
+        put(HIDX, (key[q] & 4095).astype(f32))
     block[pl.ds(SIDX, S), :] = slot_place.astype(f32)[0:S]
     block[pl.ds(SIDX + S, ROWS - SIDX - S), :] = jnp.zeros((ROWS - SIDX - S, 128), f32)
 
@@ -322,7 +338,7 @@
 def rounds(
     data, local, vel_in, water, out, water_out,
     w, g, m, prow, plane, crow, clane, cont, pf, pb, x, xt, wc, d, length, scale, delta,
-    sw, sm, srow, slane, sww, sx, sxt, sd, slength, sscale, sdelta, vel, vel_sem, water_sem,
+    sw, sm, srow, slane, sww, sx, sxt, sd, slength, sscale, sdelta, wx, vel, vel_sem, water_sem,
 ):
     load = pltpu.make_async_copy(vel_in, vel, vel_sem)
     load.start()
@@ -381,10 +397,16 @@
         [crow[r] for r in range(E)],
         [clane[r] for r in range(E)],
     )
+    given = [rows_at(base + B * k, B) for base in (DIFF, DVEL) for k in range(3)]
+    half = [data[:, HIDX + r, :].astype(i32) for r in range(E)]
+    given = pick(
+        given + [rows_at(SCALE, B)], [(h >> 7) & 15 for h in half], [h & 127 for h in half]
+    )
     for r in range(E):
-        diff = [data[:, DIFF + E * k + r, :] for k in range(3)]
-        dvel = [data[:, DVEL + E * k + r, :] for k in range(3)]
-        s = data[:, SCALE + r, :]
+        sign = jnp.where(half[r] < 2048, 1.0, -1.0)
+        diff = [sign * given[k][r] for k in range(3)]
+        dvel = [sign * given[3 + k][r] for k in range(3)]
+        s = given[6][r]
         far, weight, moved, first = geometry(diff, dvel, s)
         for k in range(3):
             w[k, r] = weight[k]
@@ -428,12 +450,12 @@
         ]
 
     def apply_k(_, carry):
+        slot_x = [sx[r] for r in range(S)]
+        cross_x = pick([slot_x], [crow[r] for r in range(E)], [clane[r] for r in range(E)])[0]
         sums = totals(
             [[w[k, r] * x[r] for r in range(E)] for k in range(3)]
             + [[g[r] * x[r] for r in range(E)]]
         )
-        slot_x = [sx[r] for r in range(S)]
-        cross_x = pick([slot_x], [crow[r] for r in range(E)], [clane[r] for r in range(E)])[0]
         slot_sum = pick([sums[3]], [srow[r] for r in range(S)], [slane[r] for r in range(S)])[0]
         z = [
             m[r] * (w[0, r] * sums[0][r] + w[1, r] * sums[1][r] + w[2, r] * sums[2][r] + g[r] * cross_x[r])
@@ -458,18 +480,27 @@
         for r in range(S):
             sxt[r] = sx[r]
         lax.fori_loop(0, ORDER, apply_k, 0)
-        sums = totals([[w[k, r] * xt[r] for r in range(E)] for k in range(3)])
         slot_xt = [sxt[r] for r in range(S)]
         cross_x = pick([slot_xt], [crow[r] for r in range(E)], [clane[r] for r in range(E)])[0]
-        slot_sum = pick(sums, [srow[r] for r in range(S)], [slane[r] for r in range(S)])
+        sums = totals([[w[k, r] * xt[r] for r in range(E)] for k in range(3)])
         for k in range(3):
             for r in range(E):
                 delta[k, r] = delta[k, r] - m[r] * (sums[k][r] + wc[k, r] * cross_x[r])
+                wx[k, r] = sums[k][r]
             for r in range(S):
-                sdelta[k, r] = sdelta[k, r] - sm[r] * (slot_sum[k][r] + sw[k, r] * slot_xt[r])
+                sdelta[k, r] = sdelta[k, r] - sm[r] * (sw[k, r] * slot_xt[r])
 
         @pl.when(index < ITER)
         def _():
+            slot_sum = pick(
+                [[wx[k, r] for r in range(E)] for k in range(3)],
+                [srow[r] for r in range(S)],
+                [slane[r] for r in range(S)],
+            )
+            for k in range(3):
+                for r in range(S):
+                    sdelta[k, r] = sdelta[k, r] - sm[r] * slot_sum[k][r]
+
             def lengthening(gap, far, s):
                 target = jnp.sqrt(2.0 * far * far - dot3(gap, gap))
                 return s * (far - target)
@@ -510,7 +541,7 @@
     passed.wait()
 
 
-CHUNKS = ((0, 72), (72, 72), (144, 64), (208, 64))
+CHUNKS = ((0, 56), (56, 56), (112, 56), (168, 56))
 
 
 def share(
@@ -552,12 +583,19 @@
     def _():
         greet(down)
 
-    peers = 1 + jnp.where(z < last, 1, 0) + jnp.where(z > 0, 1, 0)
+    @pl.when(z == 0)
+    def _():
+        greet(me + 2 * last)
+
+    @pl.when(z == last)
+    def _():
+        greet(me - 2 * last)
+
+    ends_of_line = jnp.where(z == 0, 1, 0) + jnp.where(z == last, 1, 0)
+    peers = 1 + jnp.where(z < last, 1, 0) + jnp.where(z > 0, 1, 0) + ends_of_line
     for load in loads[:6]:
         load.wait()
-    prepare(
-        pos, vel, mass, bonds, left, right, block, local, table, ends, keys, atoms, before, slots
-    )
+    bonds_as_given(pos, vel, mass, bonds, left, right, block, table, ends, slots)
     pl.semaphore_wait(barrier, peers)
 
     def copy(origin, source, k, target, sem):
@@ -571,8 +609,6 @@
             device_id_type=pl.DeviceIdType.MESH,
         )
 
-    here = pltpu.make_async_copy(block, out.at[me], local_sem)
-    here.start()
     sent = []
 
     def push(when, origin, source, k, target, sem):
@@ -582,15 +618,16 @@
         def _():
             copy(origin, source, k, target, sem).start()
 
-    for k in range(len(CHUNKS)):
-        push(z < last, block, me, k, up, 0)
-        push(z > 0, block, me, k, down, 1)
-        push(z >= 0, block, me, k, partner, 2)
-    for load in loads[6:]:
-        load.wait()
-    waters(wpos, wvel, wout, water)
-    for away in range(1, last + 1):
-        for k in range(len(CHUNKS)):
+    def give(chunks):
+        for k in chunks:
+            push(z == 0, block, me, k, me + 2 * last, 15)
+            push(z == last, block, me, k, me - 2 * last, 16)
+            push(z < last, block, me, k, up, 0)
+            push(z > 0, block, me, k, down, 1)
+            push(z >= 0, block, me, k, partner, 2)
+
+    def relay(away, chunks):
+        for k in chunks:
             for side, arrives, source, onward, target in (
                 (0, z >= away, me - 2 * away, z < last, up),
                 (1, z + away <= last, me + 2 * away, z > 0, down),
@@ -601,9 +638,26 @@
                 def _(source=source, k=k):
                     copy(out.at[source], source, k, partner, 0).wait_recv()
 
-                if away < last:
+                if away < last - 1:
                     push(arrives & onward, out.at[source], source, k, target, sem)
                 push(arrives, out.at[source], source, k, partner, sem + 1)
+
+    early, late = (0, 1), (2, 3)
+    give(early)
+    order_bonds(ends, before)
+    relay(1, early)
+    use_order(block, local, table, ends, keys, atoms, before, slots)
+    give(late)
+    here = pltpu.make_async_copy(block, out.at[me], local_sem)
+    here.start()
+    relay(2, early)
+    for load in loads[6:]:
+        load.wait()
+    waters(wpos, wvel, wout, water)
+    for away in range(3, last + 1):
+        relay(away, early)
+    for away in range(1, last + 1):
+        relay(away, late)
     for k in range(len(CHUNKS)):
         for chip in range(last + 1):
             source = 2 * chip + 1 - core
@@ -649,7 +703,7 @@
             pltpu.VMEM((32, 128), i32),
             pltpu.VMEM((8, 128), i32),
             pltpu.VMEM((18, 8, 128), f32),
-            pltpu.SemaphoreType.DMA((4 * count // 2, len(CHUNKS))),
+            pltpu.SemaphoreType.DMA((17, len(CHUNKS))),
             pltpu.SemaphoreType.DMA((count, len(CHUNKS))),
             pltpu.SemaphoreType.DMA,
             pltpu.SemaphoreType.DMA((8,)),
@@ -681,6 +735,7 @@
         ((3, E), f32), ((3, E), f32), ((E,), f32), ((E,), f32), ((3, E), f32),
         ((3, S), f32), ((S,), f32), ((S,), i32), ((S,), i32), ((S,), f32),
         ((S,), f32), ((S,), f32), ((3, S), f32), ((S,), f32), ((S,), f32), ((3, S), f32),
+        ((3, E), f32),
     ]
     protein_velocity, water_velocity = pl.pallas_call(
         rounds,

time: 42.5 us -> 40.4 us (0.951)
  Pallas kernels: 41.7 us -> 39.6 us
    pallas_call x1, Pallas kernels: 21.4 us -> 19.2 us  [on_device(): pl.pallas_call(share, out_shape=(jax.ShapeDtypeStruct((count, ROWS, 128),...]
where the time goes in v4:
time: 40.4 us; the launch traced here: 40.2 us
  Pallas kernels  39.6 us (98%)
  between operations  0.64 us (2%)
    pallas_call x1, Pallas kernels, on_device(): pl.pallas_call(rounds, out_shape=(jax.ShapeDtypeStruct(protein_vel.shape,...  20.4 us
    pallas_call x1, Pallas kernels, on_device(): pl.pallas_call(share, out_shape=(jax.ShapeDtypeStruct((count, ROWS, 128),...  19.2 us

profile of v4, /device:TPU:1, one launch (start us, length us, event | category | flops | bytes accessed | tf_op | source)
XLA Modules:
  0.0 40.2 jit_solution(3515994456842731217)
XLA Ops:
  0.6 19.2 %share.1 = (f32[8,224,128]{2,1,0:T(8,128)S(1)}, f32[32,128]{1,0:T(8,128)S(1)}, f32[9,1024]{1,0:T(8,128)S(1)}) custom-call(f32[3,2048]{1,0:T(4,128)} %pos_in.1, f32[3,2048]{1,0:T(4,128)} %vel_in.3, f32[16,128]{1,0:T(8,128)} %bitcast.3, s32[2,1280]{1,0:T(2,128)} %bonds_in.1, s32[3,128]{1,0:T(4,128)} %bitcast.4, s32[3,128]{1,0:T(4,128)} %bitcast.5, ...), custom_call_target="tpu_custom_call" | custom-call | tf_op jit(solution)/shard_map/share/pallas_call | solution.py:680
  19.8 20.4 %rounds.1 = (f32[3,2048]{1,0:T(4,128)}, f32[9,1024]{1,0:T(8,128)}) custom-call(f32[8,224,128]{2,1,0:T(8,128)S(1)} %get-tuple-element.5.data, f32[32,128]{1,0:T(8,128)S(1)} %get-tuple-element.6.local, f32[3,2048]{1,0:T(4,128)} %vel_in.3, f32[9,1024]{1,0:T(8,128)S(1)} %get-tuple-element.7.water), custom_call_target="tpu_custom_call" | custom-call | tf_op jit(solution)/shard_map/rounds/pallas_call | solution.py:740

commit v5 on v4

--- a/solution.py
+++ b/solution.py
@@ -1,3 +1,4 @@
+import functools
 import math
 
 import jax
@@ -27,6 +28,7 @@
 SVEL, SMASS = SPOS + 3 * S, SPOS + 6 * S
 EARLY = SPOS + 7 * S
 E = 20
+PANEL = 7
 MASS, PIDX, CONT, CIDX, HIDX = EARLY, EARLY + E, EARLY + 2 * E, EARLY + 3 * E, EARLY + 4 * E
 SIDX = EARLY + 5 * E
 ROWS = 224
@@ -204,62 +206,9 @@
         block[pl.ds(SPOS + S * k, S), :] = at[4][k][0:S]
 
 
-def order_bonds(ends, before):
+def order_bonds(ends, before, local, slots):
     lane = lax.broadcasted_iota(i32, (8, 128), 1)
     sub = lax.broadcasted_iota(i32, (8, 128), 0)
-    start = []
-    for q in range(4):
-        at = sub + 8 * q
-        start.append((ends[pl.ds(8 * q, 8), :] << 12) | (at << 7) | lane)
-    done = sort4(start)
-    for q in range(4):
-        before[pl.ds(8 * q, 8), :] = done[q]
-
-
-def use_order(block, local, table, ends, keys, atoms, before, slots):
-    lane = lax.broadcasted_iota(i32, (8, 128), 1)
-    sub = lax.broadcasted_iota(i32, (8, 128), 0)
-    rows, lanes = [], []
-    for q in range(3):
-        n = jnp.minimum(lane * E + sub + 8 * q, 4095)
-        rows.append(((n & 3) << 3) | ((n >> 2) & 7))
-        lanes.append(n >> 5)
-    key = [g[0] for g in gather_rows([row_of(before)], 32, rows, lanes)]
-    for q in range(3):
-        keys[pl.ds(8 * q, 8), :] = key[q]
-    atom = [k >> 12 for k in key]
-    twin = [(k & 4095) ^ 2048 for k in key]
-    other = [
-        g[0]
-        for g in gather_rows([row_of(ends)], 26, [t >> 7 for t in twin], [t & 127 for t in twin])
-    ]
-
-    slot_atom = slots[...]
-    own_atom = [(sub + 8 * q) * 128 + lane for q in range(2)]
-    queries = [(other[q] << 12) | twin[q] for q in range(3)]
-    queries += [(a << 12) | 4095 for a in [slot_atom] + own_atom]
-    leaders = jnp.broadcast_to(keys[pl.ds(0, 1), :], (8, 128))
-    found_row, found_lane, found_key = [], [], []
-    for query in queries:
-        low = jnp.zeros((8, 128), i32)
-        for bit in (64, 32, 16, 8, 4, 2, 1):
-            low = jnp.where(take(leaders, low + bit) <= query, low + bit, low)
-        count = jnp.full((8, 128), -1, i32)
-        best = jnp.full((8, 128), -1, i32)
-        for r in range(E):
-            seen = take(jnp.broadcast_to(keys[pl.ds(r, 1), :], (8, 128)), low)
-            less = seen <= query
-            count = jnp.where(less, count + 1, count)
-            best = jnp.where(less, seen, best)
-        found_row.append(count)
-        found_lane.append(low)
-        found_key.append(best)
-    places = [found_row[q] * 128 + found_lane[q] for q in range(6)]
-    slot_place = jnp.where((found_key[3] >> 12) == slot_atom, places[3], -1)
-    for q in range(2):
-        place = jnp.where((found_key[4 + q] >> 12) == own_atom[q], places[4 + q], -1)
-        local[pl.ds(8 * q, 8), :] = place.astype(f32)
-
     high = lax.broadcasted_iota(i32, (16, 128), 0)
     code = lax.broadcasted_iota(i32, (16, 128), 1) + 1
     low_of = lax.broadcasted_iota(i32, (128, 128), 0)
@@ -280,11 +229,85 @@
     local[pl.ds(16, 16), :] = jnp.where(
         which[0:16] > 0.0, which[16:32] * 128.0 + which[0:16] - 129.0, -1.0
     )
+    atom = [ends[pl.ds(8 * q, 8), :] for q in range(4)]
+    slot = gather_rows(
+        [row_of(local.at[pl.ds(16, 16)])], 16, [a >> 7 for a in atom], [a & 127 for a in atom]
+    )
+    start = []
+    for q in range(4):
+        inner = jnp.where((slot[q][0] >= 0.0) & (atom[q] < 2048), 0, 1 << 24)
+        start.append(inner | (atom[q] << 12) | ((sub + 8 * q) << 7) | lane)
+    done = sort4(start)
+    for q in range(4):
+        before[pl.ds(8 * q, 8), :] = done[q]
+
+
+def use_order(block, local, table, ends, keys, atoms, before, slots):
+    lane = lax.broadcasted_iota(i32, (8, 128), 1)
+    sub = lax.broadcasted_iota(i32, (8, 128), 0)
+    rows, lanes = [], []
+    for q in range(3):
+        row = sub + 8 * q
+        n = jnp.where(
+            row < PANEL,
+            lane * PANEL + row,
+            jnp.minimum(lane * (E - PANEL) + row + PANEL * 127, 4095),
+        )
+        rows.append(((n & 3) << 3) | ((n >> 2) & 7))
+        lanes.append(n >> 5)
+    key = [g[0] for g in gather_rows([row_of(before)], 32, rows, lanes)]
+    for q in range(3):
+        keys[pl.ds(8 * q, 8), :] = key[q]
+    atom = [(k >> 12) & 4095 for k in key]
+    twin = [(k & 4095) ^ 2048 for k in key]
+    other = [
+        g[0]
+        for g in gather_rows([row_of(ends)], 26, [t >> 7 for t in twin], [t & 127 for t in twin])
+    ]
+
+    slot_atom = slots[...]
+    own_atom = [(sub + 8 * q) * 128 + lane for q in range(2)]
+    slots_of = row_of(local.at[pl.ds(16, 16)])
+    far_slot = gather_rows([slots_of], 16, [a >> 7 for a in other], [a & 127 for a in other])
+    far_inner = [jnp.where(g[0] >= 0.0, 0, 1 << 24) for g in far_slot]
+    own_inner = [jnp.where(local[pl.ds(16 + 8 * q, 8), :] >= 0.0, 0, 1 << 24) for q in range(2)]
+    queries = [far_inner[q] | (other[q] << 12) | twin[q] for q in range(3)]
+    queries += [(slot_atom << 12) | 4095]
+    queries += [own_inner[q] | (own_atom[q] << 12) | 4095 for q in range(2)]
+    leaders = [jnp.broadcast_to(keys[pl.ds(r, 1), :], (8, 128)) for r in (0, PANEL)]
+    border = take(leaders[1], jnp.zeros((8, 128), i32))
+    found_row, found_lane, found_key = [], [], []
+    for query in queries:
+        low = jnp.zeros((8, 128), i32)
+        second = query >= border
+        for bit in (64, 32, 16, 8, 4, 2, 1):
+            leader = jnp.where(second, take(leaders[1], low + bit), take(leaders[0], low + bit))
+            low = jnp.where(leader <= query, low + bit, low)
+        count = jnp.where(second, PANEL - 1, -1)
+        best = jnp.full((8, 128), -1, i32)
+        for r in range(E):
+            seen = take(jnp.broadcast_to(keys[pl.ds(r, 1), :], (8, 128)), low)
+            less = (seen <= query) & (second if r >= PANEL else ~second)
+            count = jnp.where(less, count + 1, count)
+            best = jnp.where(less, seen, best)
+        found_row.append(count)
+        found_lane.append(low)
+        found_key.append(best)
+    places = [found_row[q] * 128 + found_lane[q] for q in range(6)]
+    slot_place = jnp.where((found_key[3] >> 12) == slot_atom, places[3], -1)
+    for q in range(2):
+        place = jnp.where(((found_key[4 + q] >> 12) & 4095) == own_atom[q], places[4 + q], -1)
+        local[pl.ds(8 * q, 8), :] = place.astype(f32)
 
     for q in range(3):
         atoms[pl.ds(8 * q, 8), :] = atom[q]
-    before[pl.ds(0, 1), :] = pltpu.roll(atoms[pl.ds(E - 1, 1), :], 1, 1)
     before[pl.ds(1, E - 1), :] = atoms[pl.ds(0, E - 1), :]
+    first_ends = pltpu.roll(atoms[pl.ds(PANEL - 1, 1), :], 1, 1)
+    second_ends = pltpu.roll(atoms[pl.ds(E - 1, 1), :], 1, 1)
+    before[pl.ds(0, 1), :] = first_ends
+    before[pl.ds(PANEL, 1), :] = jnp.where(
+        lax.broadcasted_iota(i32, (1, 128), 1) == 0, first_ends, second_ends
+    )
     own_rows, own_lanes = [a >> 7 for a in atom], [a & 127 for a in atom]
     own = gather_rows([row_of(table, 6), row_of(local.at[pl.ds(16, 16)])], 16, own_rows, own_lanes)
     for q in range(3):
@@ -338,7 +361,7 @@
 def rounds(
     data, local, vel_in, water, out, water_out,
     w, g, m, prow, plane, crow, clane, cont, pf, pb, x, xt, wc, d, length, scale, delta,
-    sw, sm, srow, slane, sww, sx, sxt, sd, slength, sscale, sdelta, wx, vel, vel_sem, water_sem,
+    sw, sm, srow, slane, sww, sx, sxt, sd, slength, sscale, sdelta, wx, cx, sz, vel, vel_sem, water_sem,
 ):
     load = pltpu.make_async_copy(vel_in, vel, vel_sem)
     load.start()
@@ -354,20 +377,37 @@
             row_ref[r] = value >> 7
             lane_ref[r] = value & 127
     keep = rows_at(CONT, E)
-    run = jnp.ones((8, 128), f32)
     for r in range(E):
         cont[r] = keep[r]
-        if r > 0:
+    first_lane = lax.broadcasted_iota(i32, (8, 128), 1) == 0
+    last_lane = lax.broadcasted_iota(i32, (8, 128), 1) == 127
+    panels = (range(PANEL), range(PANEL, E))
+    whole = []
+    for panel in panels:
+        run = jnp.ones((8, 128), f32)
+        for r in panel:
+            if r > panel[0]:
+                run = run * keep[r]
+            pf[r] = run
+        whole.append(run)
+        run = jnp.ones((8, 128), f32)
+        for r in reversed(panel):
+            pb[r] = run
             run = run * keep[r]
-        pf[r] = run
-    whole = run
-    run = jnp.ones((8, 128), f32)
-    for r in range(E - 1, -1, -1):
-        pb[r] = run
-        run = run * keep[r]
-    extra = jnp.max(jnp.sum(whole, axis=1, keepdims=True)).astype(i32)
-    opens = keep[0]
-    closes = pltpu.roll(opens, 127, 1)
+    extra = jnp.max(jnp.sum(whole[0] + whole[1], axis=1, keepdims=True)).astype(i32)
+
+    def from_left(ends):
+        one, two = (pltpu.roll(part, 1, 1) for part in ends)
+        return [keep[0] * one, keep[PANEL] * jnp.where(first_lane, one, two)]
+
+    def from_right(starts):
+        one, two = (pltpu.roll(keep[panel[0]] * part, 127, 1) for panel, part in zip(panels, starts))
+        return [jnp.where(last_lane, two, one), jnp.where(last_lane, 0.0, two)]
+
+    spilt = data[:, CIDX + PANEL, :]
+    for r in range(PANEL + 1, E):
+        spilt = jnp.maximum(spilt, data[:, CIDX + r, :])
+    spilt = jnp.max(spilt) >= 0.0
 
     def geometry(diff, dvel, s):
         far = jnp.sqrt(dot3(diff, diff))
@@ -392,10 +432,31 @@
         slength[r] = far
         sscale[r] = s
         sx[r] = first
-    near = pick(
-        [[sw[k, r] for r in range(S)] for k in range(3)],
-        [crow[r] for r in range(E)],
-        [clane[r] for r in range(E)],
+    def to_entries(tables, refs):
+        for some, when in ((range(PANEL), None), (range(PANEL, E), spilt)):
+
+            def fill(some=some):
+                got = pick(
+                    [[part() for part in table] for table in tables],
+                    [crow[r] for r in some],
+                    [clane[r] for r in some],
+                )
+                for ref, part in zip(refs, got):
+                    for r, value in zip(some, part):
+                        ref[r] = value
+
+            if when is None:
+                fill()
+            else:
+                pl.when(when)(fill)
+
+    for r in range(PANEL, E):
+        cx[r] = jnp.zeros((8, 128), f32)
+        for k in range(3):
+            wc[k, r] = jnp.zeros((8, 128), f32)
+    to_entries(
+        [[functools.partial(lambda k, r: sw[k, r], k, r) for r in range(S)] for k in range(3)],
+        [wc.at[k] for k in range(3)],
     )
     given = [rows_at(base + B * k, B) for base in (DIFF, DVEL) for k in range(3)]
     half = [data[:, HIDX + r, :].astype(i32) for r in range(E)]
@@ -411,57 +472,75 @@
         for k in range(3):
             w[k, r] = weight[k]
             d[k, r] = moved[k]
-            wc[k, r] = near[k][r]
             delta[k, r] = jnp.zeros((8, 128), f32)
-        g[r] = dot3(weight, [near[k][r] for k in range(3)])
+        g[r] = dot3(weight, [wc[k, r] for k in range(3)])
         m[r] = data[:, MASS + r, :]
         length[r] = far
         scale[r] = s
         x[r] = first
 
     def totals(parts):
-        count = len(parts)
         inside = []
         for part in parts:
-            acc = part[0]
-            fwd = [acc]
-            for r in range(1, E):
-                acc = part[r] + cont[r] * acc
-                fwd.append(acc)
-            for r in range(E - 2, -1, -1):
-                fwd[r] = jnp.where(cont[r + 1] > 0.0, fwd[r + 1], fwd[r])
+            fwd = list(part)
+            for panel in panels:
+                for r in panel[1:]:
+                    fwd[r] = part[r] + cont[r] * fwd[r - 1]
+                for r in reversed(panel[:-1]):
+                    fwd[r] = jnp.where(cont[r + 1] > 0.0, fwd[r + 1], fwd[r])
             inside.append(fwd)
-        ahead = tuple(opens * pltpu.roll(part[E - 1], 1, 1) for part in inside)
-        back = tuple(closes * pltpu.roll(part[0], 127, 1) for part in inside)
+        start = []
+        for part in inside:
+            start += from_left([part[PANEL - 1], part[E - 1]])
+            start += from_right([part[0], part[PANEL]])
 
         def spread(_, now):
-            ahead_now, back_now = now[:count], now[count:]
-            new = [ahead[k] + opens * pltpu.roll(whole * ahead_now[k], 1, 1) for k in range(count)]
-            new += [back[k] + closes * pltpu.roll(whole * back_now[k], 127, 1) for k in range(count)]
+            new = []
+            for k in range(0, len(start), 4):
+                left = from_left([whole[0] * now[k], whole[1] * now[k + 1]])
+                right = from_right([whole[0] * now[k + 2], whole[1] * now[k + 3]])
+                new += [a + b for a, b in zip(start[k : k + 4], left + right)]
             return tuple(new)
 
-        carried = lax.fori_loop(0, extra, spread, ahead + back)
-        return [
-            [
-                inside[k][r] + pf[r] * carried[k] + pb[r] * carried[count + k]
-                for r in range(E)
-            ]
-            for k in range(count)
-        ]
+        carried = lax.fori_loop(0, extra, spread, tuple(start))
+        out = []
+        for k, part in enumerate(inside):
+            left, right = carried[4 * k : 4 * k + 2], carried[4 * k + 2 : 4 * k + 4]
+            out.append(
+                [
+                    part[r] + pf[r] * left[r >= PANEL] + pb[r] * right[r >= PANEL]
+                    for r in range(E)
+                ]
+            )
+        return out
+
+    def to_slots(parts, refs):
+        rows, lanes = [srow[r] for r in range(S)], [slane[r] for r in range(S)]
+        got = pick([part[:PANEL] for part in parts], rows, lanes)
+        for ref, part in zip(refs, got):
+            for r in range(S):
+                ref[r] = part[r]
+
+        @pl.when(spilt)
+        def _():
+            rest = pick([part[PANEL:] for part in parts], [row - PANEL for row in rows], lanes)
+            for ref, part in zip(refs, rest):
+                for r in range(S):
+                    ref[r] = ref[r] + part[r]
 
     def apply_k(_, carry):
         slot_x = [sx[r] for r in range(S)]
-        cross_x = pick([slot_x], [crow[r] for r in range(E)], [clane[r] for r in range(E)])[0]
+        to_entries([[functools.partial(lambda r: sx[r], r) for r in range(S)]], [cx])
         sums = totals(
             [[w[k, r] * x[r] for r in range(E)] for k in range(3)]
             + [[g[r] * x[r] for r in range(E)]]
         )
-        slot_sum = pick([sums[3]], [srow[r] for r in range(S)], [slane[r] for r in range(S)])[0]
+        to_slots([sums[3]], [sz.at[0]])
         z = [
-            m[r] * (w[0, r] * sums[0][r] + w[1, r] * sums[1][r] + w[2, r] * sums[2][r] + g[r] * cross_x[r])
+            m[r] * (w[0, r] * sums[0][r] + w[1, r] * sums[1][r] + w[2, r] * sums[2][r] + g[r] * cx[r])
             for r in range(E)
         ]
-        slot_z = [sm[r] * (slot_sum[r] + sww[r] * slot_x[r]) for r in range(S)]
+        slot_z = [sm[r] * (sz[0, r] + sww[r] * slot_x[r]) for r in range(S)]
         slot_twin = swap(slot_z)
         for r in range(S):
             new = slot_x[r] - (slot_z[r] + slot_twin[r])
@@ -481,25 +560,21 @@
             sxt[r] = sx[r]
         lax.fori_loop(0, ORDER, apply_k, 0)
         slot_xt = [sxt[r] for r in range(S)]
-        cross_x = pick([slot_xt], [crow[r] for r in range(E)], [clane[r] for r in range(E)])[0]
+        to_entries([[functools.partial(lambda r: sxt[r], r) for r in range(S)]], [cx])
         sums = totals([[w[k, r] * xt[r] for r in range(E)] for k in range(3)])
         for k in range(3):
             for r in range(E):
-                delta[k, r] = delta[k, r] - m[r] * (sums[k][r] + wc[k, r] * cross_x[r])
+                delta[k, r] = delta[k, r] - m[r] * (sums[k][r] + wc[k, r] * cx[r])
                 wx[k, r] = sums[k][r]
             for r in range(S):
                 sdelta[k, r] = sdelta[k, r] - sm[r] * (sw[k, r] * slot_xt[r])
 
         @pl.when(index < ITER)
         def _():
-            slot_sum = pick(
-                [[wx[k, r] for r in range(E)] for k in range(3)],
-                [srow[r] for r in range(S)],
-                [slane[r] for r in range(S)],
-            )
+            to_slots([[wx[k, r] for r in range(E)] for k in range(3)], [sz.at[k] for k in range(3)])
             for k in range(3):
                 for r in range(S):
-                    sdelta[k, r] = sdelta[k, r] - sm[r] * slot_sum[k][r]
+                    sdelta[k, r] = sdelta[k, r] - sm[r] * sz[k, r]
 
             def lengthening(gap, far, s):
                 target = jnp.sqrt(2.0 * far * far - dot3(gap, gap))
@@ -644,7 +719,7 @@
 
     early, late = (0, 1), (2, 3)
     give(early)
-    order_bonds(ends, before)
+    order_bonds(ends, before, local, slots)
     relay(1, early)
     use_order(block, local, table, ends, keys, atoms, before, slots)
     give(late)
@@ -735,7 +810,7 @@
         ((3, E), f32), ((3, E), f32), ((E,), f32), ((E,), f32), ((3, E), f32),
         ((3, S), f32), ((S,), f32), ((S,), i32), ((S,), i32), ((S,), f32),
         ((S,), f32), ((S,), f32), ((3, S), f32), ((S,), f32), ((S,), f32), ((3, S), f32),
-        ((3, E), f32),
+        ((3, E), f32), ((E,), f32), ((3, S), f32),
     ]
     protein_velocity, water_velocity = pl.pallas_call(
         rounds,

time: 40.4 us -> 40.2 us (level)
    pallas_call x1, Pallas kernels: 20.4 us -> 19.8 us  [on_device(): pl.pallas_call(rounds, out_shape=(jax.ShapeDtypeStruct(protein_vel.shape,...]
where the time goes in v5:
time: 40.2 us; the launch traced here: 40.1 us
  Pallas kernels  39.4 us (98%)
  between operations  0.64 us (2%)
    pallas_call x1, Pallas kernels, on_device(): pl.pallas_call(rounds, out_shape=(jax.ShapeDtypeStruct(protein_vel.shape,...  19.8 us
    pallas_call x1, Pallas kernels, on_device(): pl.pallas_call(share, out_shape=(jax.ShapeDtypeStruct((count, ROWS, 128),...  19.6 us

profile of v5, /device:TPU:1, one launch (start us, length us, event | category | flops | bytes accessed | tf_op | source)
XLA Modules:
  0.0 40.1 jit_solution(9110244326200917211)
XLA Ops:
  0.6 19.6 %share.1 = (f32[8,224,128]{2,1,0:T(8,128)S(1)}, f32[32,128]{1,0:T(8,128)S(1)}, f32[9,1024]{1,0:T(8,128)S(1)}) custom-call(f32[3,2048]{1,0:T(4,128)} %pos_in.1, f32[3,2048]{1,0:T(4,128)} %vel_in.3, f32[16,128]{1,0:T(8,128)} %bitcast.3, s32[2,1280]{1,0:T(2,128)} %bonds_in.1, s32[3,128]{1,0:T(4,128)} %bitcast.4, s32[3,128]{1,0:T(4,128)} %bitcast.5, ...), custom_call_target="tpu_custom_call" | custom-call | tf_op jit(solution)/shard_map/share/pallas_call | solution.py:755
  20.2 19.8 %rounds.1 = (f32[3,2048]{1,0:T(4,128)}, f32[9,1024]{1,0:T(8,128)}) custom-call(f32[8,224,128]{2,1,0:T(8,128)S(1)} %get-tuple-element.5.data, f32[32,128]{1,0:T(8,128)S(1)} %get-tuple-element.6.local, f32[3,2048]{1,0:T(4,128)} %vel_in.3, f32[9,1024]{1,0:T(8,128)S(1)} %get-tuple-element.7.water), custom_call_target="tpu_custom_call" | custom-call | tf_op jit(solution)/shard_map/rounds/pallas_call | solution.py:815
